TPU v7x, 32 devices: a whole 2x2x4 slice. The times are simulated.
32 devices in a mesh: tm: 8 (over y, x, core), space: 4 (over z).
Axes of the slice: x: 2, y: 2, z: 4, core: 2. Of those that a mesh axis runs over, the one named last changes fastest.
Arguments:
- rhs: float32 [16, 1024, 1024], P('tm', 'space'), may hold values from -6 to 6
- guess: float32 [16, 1024, 1024], P('tm', 'space'), may hold values from -6 to 6
- diffusion: float32 [1024, 1024], P('space'), may hold values from 0.2 to 2
Outputs:
- solution: float32 [16, 1024, 1024], P('tm', 'space')
- norms: float32 [6], replicated
All inputs are finite; a program needn't handle non-finite values.
Results may differ from a plain program's by a relative error of at most 0.0001.
Values sent between devices are 32-bit elements; how exact they have to be, the bound alone decides.
A program may use at most 64 MiB of HBM per device.

v0:
```python
import functools

import jax
import jax.numpy as jnp
from jax import lax
from jax.experimental import pallas as pl
from jax.experimental.pallas import tpu as pltpu
from jax.sharding import PartitionSpec as P

LEVELS = 5


damping = 0.8


def with_halo(block, sides, width):
    for axis, dim in sides:
        count = lax.axis_size(axis)
        forward = [(i, i + 1) for i in range(count - 1)]
        backward = [(target, source) for source, target in forward]
        low = lax.ppermute(
            lax.slice_in_dim(block, block.shape[dim] - width, None, axis=dim), axis, forward
        )
        high = lax.ppermute(lax.slice_in_dim(block, 0, width, axis=dim), axis, backward)
        block = jnp.concatenate([low, block, high], axis=dim)
    return block


def shifted(value, axis, steps):
    count = lax.axis_size(axis)
    first, last = (max(0, -steps), min(count, count - steps))
    return lax.ppermute(value, axis, [(source, source + steps) for source in range(first, last)])


def from_partner(value, axis, apart):
    mask = 2**apart
    pairs = [(source, source ^ mask) for source in range(lax.axis_size(axis))]
    return lax.ppermute(value, axis, pairs)


def neighbours(field):
    rows = with_halo(field, (("space", 1),), 1)
    padded = jnp.pad(rows, ((0, 0), (0, 0), (1, 1)))
    total = padded[:, 2:, 1:-1] + padded[:, :-2, 1:-1]
    total = total + padded[:, 1:-1, 2:] + padded[:, 1:-1, :-2]
    return total


def residual(field, source, scaled, diag, stride):
    earlier = shifted(field[-1:], "tm", stride)
    before = jnp.concatenate([earlier, field[:-1]], axis=0)
    image = diag * field - scaled * neighbours(field) - before
    return source - image


def stride_of(level):
    if level == 0:
        return 1
    return 2 ** (level - 1)


def body(rhs, guess, diffusion):
    position = lax.axis_index("tm")
    cells = rhs.shape[1] * lax.axis_size("space") * rhs.shape[2]
    partials = []

    def weight_of(level):
        if level <= 1:
            return jnp.float32(1.0)
        stride = stride_of(level)
        return jnp.where(position % stride == stride - 1, 1.0, 0.0).astype(jnp.float32)

    def record(resid, level):
        local_part = jnp.sum(resid * resid) * weight_of(level)
        partials.append(local_part)

    sources = [rhs]
    fields = []
    field = guess
    for level in range(LEVELS - 1):
        source = sources[level]
        scaled = 2.0**level * diffusion
        diag = 1.0 + 4.0 * scaled
        stride = stride_of(level)
        if level == 0:
            field = field + damping * residual(field, source, scaled, diag, stride) / diag
        else:
            field = damping * source / diag
        resid = residual(field, source, scaled, diag, stride)
        record(resid, level)
        fields.append(field)
        if level == 0:
            coarse = resid[0:1] + resid[1:2]
        else:
            coarse = resid + from_partner(resid, "tm", level - 1)
        sources.append(coarse)
    level = LEVELS - 1
    source = sources[level]
    scaled = 2.0**level * diffusion
    diag = 1.0 + 4.0 * scaled
    stride = stride_of(level)
    field = damping * source / diag
    field = field + damping * residual(field, source, scaled, diag, stride) / diag
    resid = residual(field, source, scaled, diag, stride)
    record(resid, level)
    correction = field
    for level in range(LEVELS - 2, -1, -1):
        scaled = 2.0**level * diffusion
        diag = 1.0 + 4.0 * scaled
        stride = stride_of(level)
        field = fields[level] + correction
        field = field + damping * residual(field, sources[level], scaled, diag, stride) / diag
        correction = field
    scaled = 1.0 * diffusion
    diag = 1.0 + 4.0 * scaled
    resid = residual(correction, rhs, scaled, diag, 1)
    record(resid, 0)
    totals = lax.psum(jnp.stack(partials), ("tm", "space"))
    norms = jnp.sqrt(totals / cells)
    return (correction, norms)


DEVICE = pl.DeviceIdType.MESH
TILE = 8
EDGE = 2 * TILE
BLOCK = 32


def cycle_kernel(
    strips, devices, cells,
    rhs_in, guess_in, diff_in, out, norms_out,
    rhs, guess, diff, v0, g1, v1, r1, v1f, sol, guess_e, v0_e, v1_e, v1f_e, sol_e,
    pair, g2h, v2, c_g2, c_v2, c_g3, c_v3, c_g4, c_v4, c_v4b, finals, weights, tile, gathered, gathered_z,
    load_sem, store_sem, zs_sem, zr_sem, ts_sem, tr_sem, ps_sem, pr_sem, as_sem, ar_sem, al_sem,
    bs_sem, br_sem, bl_sem, rs_sem, credit, ns_sem, nr_sem, ms_sem, mr_sem,
):
    me = lax.axis_index("tm")
    strip = lax.axis_index("space")
    rows, width = rhs_in.shape[1], rhs_in.shape[2]
    chips = devices // 2
    core = lax.rem(me, 2)
    chip = me // 2
    low, high = EDGE, EDGE + rows
    first, last = me == 0, me == devices - 1
    top, bottom = strip == 0, strip == strips - 1
    piece = rows // devices

    def aligned(value):
        return pl.multiple_of(value, TILE)

    def tm_copy(src, dst, send, recv, target):
        return pltpu.make_async_remote_copy(
            src_ref=src, dst_ref=dst, send_sem=send, recv_sem=recv,
            device_id={"tm": target, "space": strip}, device_id_type=DEVICE,
        )

    def space_copy(src, dst, send, recv, target):
        return pltpu.make_async_remote_copy(
            src_ref=src, dst_ref=dst, send_sem=send, recv_sem=recv,
            device_id={"tm": me, "space": target}, device_id_type=DEVICE,
        )

    later = jnp.minimum(me + 1, devices - 1)
    loads = [
        pltpu.make_async_copy(guess_in, guess.at[:, low:high], load_sem.at[0]),
        pltpu.make_async_copy(diff_in, diff.at[low:high], load_sem.at[1]),
        pltpu.make_async_copy(rhs_in, rhs.at[:, low:high], load_sem.at[2]),
    ]
    for copy in loads:
        copy.start()

    barrier = pltpu.get_barrier_semaphore()
    for i in range(1, devices):
        pl.semaphore_signal(
            barrier, inc=1, device_id={"tm": lax.rem(me + i, devices), "space": strip}, device_id_type=DEVICE
        )
    for i in range(1, strips):
        pl.semaphore_signal(
            barrier, inc=1, device_id={"tm": me, "space": lax.rem(strip + i, strips)}, device_id_type=DEVICE
        )
    pl.semaphore_wait(barrier, devices + strips - 2)

    down = jnp.minimum(strip + 1, strips - 1)
    up = jnp.maximum(strip - 1, 0)

    def halo_pair(index, tail, head, low_dst, high_dst):
        return (
            space_copy(tail, low_dst, zs_sem.at[index, 0], zr_sem.at[index, 0], down),
            space_copy(head, high_dst, zs_sem.at[index, 1], zr_sem.at[index, 1], up),
        )

    before_low, after_high = slice(low - TILE, low), slice(high, high + TILE)
    halos = [
        halo_pair(
            0, guess_in.at[:, rows - TILE:rows], guess_in.at[:, 0:TILE],
            guess.at[:, before_low], guess.at[:, after_high],
        ),
        halo_pair(
            1, diff_in.at[rows - TILE:rows], diff_in.at[0:TILE], diff.at[before_low], diff.at[after_high],
        ),
        halo_pair(
            2, rhs_in.at[:, rows - TILE:rows], rhs_in.at[:, 0:TILE],
            rhs.at[:, before_low], rhs.at[:, after_high],
        ),
    ]

    def start_halo(pair_of):
        @pl.when(jnp.logical_not(bottom))
        def _():
            pair_of[0].start()

        @pl.when(jnp.logical_not(top))
        def _():
            pair_of[1].start()

    def finish_halo(pair_of):
        @pl.when(jnp.logical_not(top))
        def _():
            pair_of[0].wait_recv()
            pair_of[1].wait_send()

        @pl.when(jnp.logical_not(bottom))
        def _():
            pair_of[1].wait_recv()
            pair_of[0].wait_send()

    for pair_of in halos:
        start_halo(pair_of)

    half = rows // 2
    quarter = rows // 4
    whole = [
        (low - TILE, quarter + TILE), (low + quarter, quarter),
        (low + 2 * quarter, quarter), (low + 3 * quarter, quarter + TILE),
    ]
    inner = [(low + quarter * j, quarter) for j in range(4)]
    guess_parts = [(low, half), (low + half, half), (low - TILE, TILE), (high, TILE)]

    def shift(stage, source, target, parts):
        return [
            tm_copy(
                source(start, size), target.at[start:start + size],
                ts_sem.at[stage, j], tr_sem.at[stage, j], later,
            )
            for j, (start, size) in enumerate(parts)
        ]

    def send(copy):
        @pl.when(jnp.logical_not(last))
        def _():
            copy.start()

    def receive(copy):
        @pl.when(jnp.logical_not(first))
        def _():
            copy.wait_recv()

    guess_shift = shift(
        0,
        lambda start, size: (
            guess.at[1, start:start + size] if size == TILE else guess_in.at[1, start - low:start - low + size]
        ),
        guess_e, guess_parts,
    )
    v0_shift = shift(1, lambda start, size: v0.at[1, start:start + size], v0_e, whole)
    v1_shift = shift(2, lambda start, size: v1.at[start:start + size], v1_e, whole)
    v1f_shift = shift(3, lambda start, size: v1f.at[start:start + size], v1f_e, whole)
    sol_shift = shift(4, lambda start, size: sol.at[1, start:start + size], sol_e, inner)
    send(guess_shift[0])
    send(guess_shift[1])

    block = [TILE]

    def at(r):
        return pl.ds(r, block[0])

    def blocks(start, size, step, init=0, ahead=0):
        def loop(begin, count, tall, carry):
            def run(i, carry):
                return step(aligned(begin + i * tall), carry)

            block[0] = tall
            if count == 1:
                carry = step(aligned(begin), carry)
            elif count:
                carry = lax.fori_loop(0, count, run, carry)
            block[0] = TILE
            return carry

        carry = loop(start, ahead // TILE, TILE, init)
        count = (size - ahead) // BLOCK
        carry = loop(start + ahead, count, BLOCK, carry)
        done = ahead + count * BLOCK
        return loop(start + done, (size - done) // TILE, TILE, carry)

    @pl.when(first)
    def _():
        def clear(r, carry):
            zero = jnp.zeros((block[0], width), jnp.float32)
            for ref in (guess_e, v0_e, v1_e, v1f_e, sol_e):
                ref[at(r), :] = zero
            v2[1, at(r), :] = zero
            return carry

        blocks(low - TILE, rows + 2 * TILE, clear, 0, TILE)

    def chunk(j, step, init=0):
        start, size = whole[j]
        return blocks(start, size, step, init, TILE if j == 0 else 0)

    def clear_edge(start):
        for ref in (guess, rhs):
            for p in range(2):
                ref[p, start:start + TILE, :] = jnp.zeros((TILE, width), jnp.float32)
        for p in range(2):
            v2[p, start:start + TILE, :] = jnp.zeros((TILE, width), jnp.float32)
        diff[start:start + TILE, :] = jnp.zeros((TILE, width), jnp.float32)

    @pl.when(top)
    def _():
        clear_edge(low - TILE)

    @pl.when(bottom)
    def _():
        clear_edge(high)

    def stencil(tall):
        size = block[0]
        lane = lax.broadcasted_iota(jnp.int32, (size, width), 1)
        not_left, not_right = lane != 0, lane != width - 1
        mid = tall[TILE:TILE + size]
        total = tall[TILE - 1:TILE + size - 1] + tall[TILE + 1:TILE + size + 1]
        total = total + jnp.where(not_left, pltpu.roll(mid, 1, 1), 0.0)
        total = total + jnp.where(not_right, pltpu.roll(mid, width - 1, 1), 0.0)
        return mid, total

    def tall_at(r):
        return pl.ds(aligned(r - TILE), block[0] + 2 * TILE)

    def coefficients(level, r):
        scaled = 2.0**level * diff[at(r), :]
        diag = 1.0 + 4.0 * scaled
        if level < 2:
            return scaled, diag, weights[level, at(r), :]
        return scaled, diag, damping / diag

    def set_weights(r, carry):
        for level in range(2):
            weights[level, at(r), :] = damping / (1.0 + 4.0 * (2.0**level * diff[at(r), :]))
        return carry

    def squares(value, keep=None):
        square = value * value
        if keep is not None:
            square = jnp.where(keep, square, 0.0)
        total = square[:, 0:128]
        for i in range(1, width // 128):
            total = total + square[:, i * 128:(i + 1) * 128]
        folded = total[0:TILE]
        for i in range(TILE, block[0], TILE):
            folded = folded + total[i:i + TILE]
        return folded

    zero_tile = jnp.zeros((TILE, 128), jnp.float32)
    keep_share = 1.0 - damping

    def sweep_last(r, carry):
        scaled, _, weight = coefficients(0, r)
        mid, total = stencil(guess[1, tall_at(r), :])
        v0[1, at(r), :] = keep_share * mid + weight * (rhs[1, at(r), :] + scaled * total + guess[0, at(r), :])
        return carry

    for copy in loads:
        copy.wait()
    blocks(low, rows, set_weights)
    for j in (1, 2):
        chunk(j, sweep_last)
        send(v0_shift[j])
    finish_halo(halos[0])
    send(guess_shift[2])
    send(guess_shift[3])
    finish_halo(halos[1])
    finish_halo(halos[2])
    blocks(low - TILE, TILE, set_weights)
    blocks(high, TILE, set_weights)
    for j in (0, 3):
        chunk(j, sweep_last)
        send(v0_shift[j])

    def sweep_first(r, carry):
        scaled, _, weight = coefficients(0, r)
        mid, total = stencil(guess[0, tall_at(r), :])
        v0[0, at(r), :] = keep_share * mid + weight * (rhs[0, at(r), :] + scaled * total + guess_e[at(r), :])
        return carry

    for copy in guess_shift:
        receive(copy)
    for j in range(4):
        chunk(j, sweep_first)

    def descend(r, carry):
        keep = jnp.logical_and(r >= low, r < high)
        scaled, diag, _ = coefficients(0, r)
        mid, total = stencil(v0[0, tall_at(r), :])
        one = rhs[0, at(r), :] - diag * mid + scaled * total + v0_e[at(r), :]
        late, total = stencil(v0[1, tall_at(r), :])
        two = rhs[1, at(r), :] - diag * late + scaled * total + mid
        source = one + two
        g1[at(r), :] = source
        _, _, weight = coefficients(1, r)
        v1[at(r), :] = weight * source
        return carry + squares(one, keep) + squares(two, keep)

    total0 = zero_tile
    for j in range(4):
        receive(v0_shift[j])
        total0 = chunk(j, descend, total0)
        send(v1_shift[j])

    def residual1(r, carry):
        keep = jnp.logical_and(r >= low, r < high)
        scaled, _, _ = coefficients(1, r)
        _, total = stencil(v1[tall_at(r), :])
        resid = keep_share * g1[at(r), :] + scaled * total + v1_e[at(r), :]
        r1[at(r), :] = resid
        return carry + squares(resid, keep)

    total1 = zero_tile
    tall_piece = piece + 2 * TILE
    c_low, c_high = EDGE, EDGE + piece
    c_rows = slice(c_low - TILE, c_high + TILE)
    sibling = me + 1 - 2 * core

    def swap_of(k):
        start = low - TILE + k * piece
        return tm_copy(
            r1.at[start:start + tall_piece], pair.at[k // 2], ps_sem.at[k // 2], pr_sem.at[k // 2], sibling
        )

    def hand_over(k):
        return tm_copy(g2h.at[k // 2], c_g2.at[chip, c_rows], as_sem.at[k // 2], ar_sem.at[chip], k)

    def join_piece(k):
        start = low - TILE + k * piece

        def join(r, carry):
            g2h[k // 2, at(r), :] = r1[at(aligned(r + start)), :] + pair[k // 2, at(r), :]
            return carry

        swap_of(k).wait_recv()
        blocks(0, tall_piece, join, 0, TILE)
        local = pltpu.make_async_copy(g2h.at[k // 2], c_g2.at[chip, c_rows], al_sem)

        @pl.when(me == k)
        def _():
            local.start()
            local.wait()

        @pl.when(me != k)
        def _():
            hand_over(k).start()

    done = 0
    for j in range(4):
        receive(v1_shift[j])
        total1 = chunk(j, residual1, total1)
        ready = (sum(whole[j]) - tall_piece - low + TILE) // piece + 1
        for k in range(done, ready):
            @pl.when(core != k % 2)
            def _():
                swap_of(k).start()
        for k in range(done, ready):
            @pl.when(core == k % 2)
            def _():
                join_piece(k)
        done = ready
    for c in range(chips):
        copy = tm_copy(g2h.at[0], c_g2.at[c, c_rows], as_sem.at[0], ar_sem.at[c], sibling)

        @pl.when(c != chip)
        def _():
            copy.wait_recv()

    has_second = jnp.logical_and(core == 0, jnp.logical_not(first))

    offset = me * piece

    def coarse_coefficients(level, r):
        return coefficients(level, aligned(r + offset))


    def coarse(step, init=0):
        return blocks(c_low - TILE, tall_piece, step, init, TILE)

    def first_sweep(level, source, field, count):
        def step(r, carry):
            _, _, weight = coarse_coefficients(level, r)
            for p in range(count):
                field[p, at(r), :] = weight * source[p, at(r), :]
            return carry

        coarse(step)

    def coarse_residual(level, source, field, target, count):
        def step(r, carry):
            keep = jnp.logical_and(r >= c_low, r < c_high)
            scaled, _, _ = coarse_coefficients(level, r)
            earlier, even = None, None
            for p in range(count):
                mid, total = stencil(field[p, tall_at(r), :])
                resid = keep_share * source[p, at(r), :] + scaled * total
                if p:
                    resid = resid + earlier
                earlier = mid
                carry = carry + squares(resid, keep)
                if p % 2 == 0:
                    even = resid
                else:
                    target[p // 2, at(r), :] = even + resid
            return carry

        return coarse(step, zero_tile)

    def ascend(level, source, field, above, target, count):
        def step(r, carry):
            scaled, _, weight = coarse_coefficients(level, r)
            earlier = None
            for p in range(count):
                mid, total = stencil(field[p, tall_at(r), :] + above[p // 2, tall_at(r), :])
                value = source[p, at(r), :] + scaled * total
                if p:
                    value = value + earlier
                earlier = mid
                target[p, at(r), :] = keep_share * mid + weight * value
            return carry

        coarse(step)

    points2, points3 = chips, chips // 2
    first_sweep(2, c_g2, c_v2, points2)
    total2 = coarse_residual(2, c_g2, c_v2, c_g3, points2)
    first_sweep(3, c_g3, c_v3, points3)
    total3 = coarse_residual(3, c_g3, c_v3, c_g4, points3)
    first_sweep(4, c_g4, c_v4, 1)

    def second_sweep(r, carry):
        scaled, _, weight = coarse_coefficients(4, r)
        mid, total = stencil(c_v4[0, tall_at(r), :])
        c_v4b[0, at(r), :] = keep_share * mid + weight * (c_g4[0, at(r), :] + scaled * total)
        return carry

    coarse(second_sweep)

    def residual4(r, carry):
        scaled, diag, _ = coarse_coefficients(4, r)
        mid, total = stencil(c_v4b[0, tall_at(r), :])
        return carry + squares(c_g4[0, at(r), :] - diag * mid + scaled * total)

    total4 = blocks(c_low, piece, residual4, zero_tile)
    c_v3f, c_v2f = finals
    ascend(3, c_g3, c_v3, c_v4b, c_v3f, points3)
    ascend(2, c_g2, c_v2, c_v3f, c_v2f, points2)

    back = []
    place = pl.ds(aligned(low + offset), piece)
    for c in range(chips):
        wants = [(0, 2 * c + core, c)]
        if c > 0:
            wants.append((1, 2 * c, c - 1))
        for kind, target, point in wants:
            src, dst = c_v2f.at[point, c_low:c_high], v2.at[kind, place]
            copy = tm_copy(src, dst, bs_sem.at[kind, c], br_sem.at[kind, me], target)
            local = pltpu.make_async_copy(src, dst, bl_sem.at[kind])
            back.append((target, copy))

            @pl.when(me == target)
            def _():
                local.start()
                local.wait()

            @pl.when(me != target)
            def _():
                copy.start()

    relays = []
    for i in range(chips):
        for side in (core, 1 - core):
            k = 2 * i + side
            rows_of = pl.ds(aligned(low + k * piece), piece)
            arrival = tm_copy(v2.at[0, rows_of], v2.at[0, rows_of], rs_sem.at[i], br_sem.at[0, k], sibling)
            relays.append((k, arrival))
    for k, arrival in relays[0::2]:
        @pl.when(k != me)
        def _():
            arrival.wait_recv()

        arrival.start()
    for k, arrival in relays[1::2]:
        arrival.wait_recv()
    for k in range(devices):
        rows_of = slice(low + k * piece, low + (k + 1) * piece)
        arrival = tm_copy(v2.at[1, rows_of], v2.at[1, rows_of], bs_sem.at[1, 0], br_sem.at[1, k], sibling)

        @pl.when(jnp.logical_and(k != me, has_second))
        def _():
            arrival.wait_recv()

    v2_halos = [
        halo_pair(
            3 + kind, v2.at[kind, high - TILE:high], v2.at[kind, low:low + TILE],
            v2.at[kind, before_low], v2.at[kind, after_high],
        )
        for kind in range(2)
    ]
    start_halo(v2_halos[0])

    @pl.when(has_second)
    def _():
        start_halo(v2_halos[1])

    sends_on = jnp.logical_and(core == 1, jnp.logical_not(last))

    @pl.when(has_second)
    def _():
        pl.semaphore_signal(credit, inc=1, device_id={"tm": me - 1, "space": strip}, device_id_type=DEVICE)

    kind = 1 - core

    def ascend1(r, carry):
        scaled, _, weight = coefficients(1, r)
        mid, total = stencil(v1[tall_at(r), :] + v2[0, tall_at(r), :])
        earlier = v1_e[at(r), :] + v2[kind, at(r), :]
        v1f[at(r), :] = keep_share * mid + weight * (g1[at(r), :] + scaled * total + earlier)
        return carry

    for j in (1, 2, 0, 3):
        if j == 0:
            finish_halo(v2_halos[0])

            @pl.when(has_second)
            def _():
                finish_halo(v2_halos[1])

        chunk(j, ascend1)
        if j == 1:
            @pl.when(sends_on)
            def _():
                pl.semaphore_wait(credit, 1)
        send(v1f_shift[j])

    def ascend_last(r, carry):
        scaled, _, weight = coefficients(0, r)
        mid, total = stencil(v0[1, tall_at(r), :] + v1f[tall_at(r), :])
        earlier = v0[0, at(r), :] + v1f[at(r), :]
        sol[1, at(r), :] = keep_share * mid + weight * (rhs[1, at(r), :] + scaled * total + earlier)
        return carry

    blocks(low - TILE, TILE, ascend_last, 0)
    for start, size in inner:
        blocks(start, size, ascend_last, 0)
    blocks(high, TILE, ascend_last, 0)

    def ascend_first(r, carry):
        scaled, _, weight = coefficients(0, r)
        mid, total = stencil(v0[0, tall_at(r), :] + v1f[tall_at(r), :])
        earlier = v0_e[at(r), :] + v1f_e[at(r), :]
        sol[0, at(r), :] = keep_share * mid + weight * (rhs[0, at(r), :] + scaled * total + earlier)
        return carry

    for j in range(4):
        receive(v1f_shift[j])

        @pl.when(jnp.logical_not(last))
        def _():
            v1f_shift[j].wait_send()
            sol_shift[j].start()

        chunk(j, ascend_first)
    stores = pltpu.make_async_copy(sol.at[:, low:high], out, store_sem)
    stores.start()

    def final_last(r, carry):
        scaled, diag, _ = coefficients(0, r)
        mid, total = stencil(sol[1, tall_at(r), :])
        return carry + squares(rhs[1, at(r), :] - diag * mid + scaled * total + sol[0, at(r), :])

    total5 = blocks(low, rows, final_last, zero_tile)

    def final_first(r, carry):
        scaled, diag, _ = coefficients(0, r)
        mid, total = stencil(sol[0, tall_at(r), :])
        return carry + squares(rhs[0, at(r), :] - diag * mid + scaled * total + sol_e[at(r), :])

    for (start, size), arrived in zip(inner, sol_shift):
        receive(arrived)
        total5 = blocks(start, size, final_first, total5)

    parts = [total0, total1, total2, total3, total4, total5]
    for level, value in enumerate(parts):
        tile[level:level + 1, :] = jnp.sum(value, axis=0, keepdims=True)
    for level in range(len(parts), TILE):
        tile[level:level + 1, :] = jnp.zeros((1, 128), jnp.float32)

    def exchange(count, own, source, slots, copier, send_sems, recv_sems):
        slots[pl.ds(own, 1)] = source[...][None]
        sent = [
            copier(source, slots.at[own], send_sems.at[i], recv_sems.at[own], lax.rem(own + i, count))
            for i in range(1, count)
        ]
        for copy in sent:
            copy.start()
        for i in range(1, count):
            other = lax.rem(own + i, count)
            copier(source, slots.at[other], send_sems.at[i], recv_sems.at[other], other).wait_recv()
        for copy in sent:
            copy.wait_send()
        total = slots[0]
        for i in range(1, count):
            total = total + slots[i]
        return total

    total = exchange(devices, me, tile, gathered, tm_copy, ns_sem, nr_sem)
    tile[...] = total
    total = exchange(strips, strip, tile, gathered_z, space_copy, ms_sem, mr_sem)
    summed = jnp.sum(total, axis=1, keepdims=True)
    norms_out[...] = jnp.broadcast_to(jnp.sqrt(summed * (1.0 / cells)), (TILE, 128))

    stores.wait()
    for group in (guess_shift, v0_shift, v1_shift, sol_shift):
        for copy in group:
            @pl.when(jnp.logical_not(last))
            def _():
                copy.wait_send()
    for _, copy in relays[0::2]:
        copy.wait_send()
    for k in range(devices):
        @pl.when(core != k % 2)
        def _():
            swap_of(k).wait_send()

        @pl.when(jnp.logical_and(core == k % 2, me != k))
        def _():
            hand_over(k).wait_send()
    for target, copy in back:
        @pl.when(me != target)
        def _():
            copy.wait_send()


def fast_body(rhs, guess, diffusion):
    devices, strips = lax.axis_size("tm"), lax.axis_size("space")
    rows, width = rhs.shape[1:]
    chips = devices // 2
    cells = rows * strips * width
    height = rows + 2 * EDGE
    c_height = rows // devices + 2 * EDGE

    def plane(*lead):
        return pltpu.VMEM(lead + (height, width), jnp.float32)

    def coarse(count):
        return pltpu.VMEM((count, c_height, width), jnp.float32)

    shared = pltpu.VMEM((chips, rows // devices + EDGE, width), jnp.float32)
    dma = pltpu.SemaphoreType.DMA
    scratch = [
        plane(2), plane(2), plane(), plane(2), plane(), plane(), plane(), plane(), plane(2),
        plane(), plane(), plane(), plane(), plane(),
        shared, shared, plane(2),
        coarse(chips), coarse(chips), coarse(chips // 2), coarse(chips // 2), coarse(1), coarse(1), coarse(1),
        (coarse(chips // 2), coarse(chips)),
        plane(2),
        pltpu.VMEM((TILE, 128), jnp.float32),
        pltpu.VMEM((devices, TILE, 128), jnp.float32),
        pltpu.VMEM((strips, TILE, 128), jnp.float32),
        dma((3,)), dma, dma((5, 2)), dma((5, 2)), dma((5, 4)), dma((5, 4)), dma((chips,)), dma((chips,)),
        dma((chips,)), dma((chips,)), dma, dma((2, devices)), dma((2, devices)), dma((2,)),
        dma((chips,)), pltpu.SemaphoreType.REGULAR,
        dma((devices,)), dma((devices,)), dma((strips,)), dma((strips,)),
    ]
    any_space = pl.BlockSpec(memory_space=pl.ANY)
    result, norms = pl.pallas_call(
        functools.partial(cycle_kernel, strips, devices, cells),
        out_shape=(
            pltpu.VMEM(rhs.shape, jnp.float32),
            jax.ShapeDtypeStruct((TILE, 128), jnp.float32),
        ),
        in_specs=[any_space] * 3,
        out_specs=(pl.BlockSpec(memory_space=pltpu.VMEM), pl.BlockSpec(memory_space=pltpu.VMEM)),
        scratch_shapes=scratch,
        compiler_params=pltpu.CompilerParams(
            collective_id=0, has_side_effects=True, vmem_limit_bytes=67_043_328 - rhs.size * 4 - 2**17
        ),
    )(rhs, guess, diffusion)
    return result, norms[:LEVELS + 1, 0]


def solution(mesh):
    in_specs = (P("tm", "space", None), P("tm", "space", None), P("space", None))
    out_specs = (P("tm", "space", None), P())

    def choose(rhs, guess, diffusion):
        points = rhs.shape[0] * lax.axis_size("tm")
        one_coarsest = points == 2 ** (LEVELS - 1) and rhs.shape[0] == 2
        even = rhs.shape[1] % (TILE * lax.axis_size("tm")) == 0 and rhs.shape[2] % 128 == 0
        if one_coarsest and even:
            return fast_body(rhs, guess, diffusion)
        return body(rhs, guess, diffusion)

    return jax.shard_map(choose, mesh=mesh, in_specs=in_specs, out_specs=out_specs, check_vma=False)
```

profile of v0, /device:TPU:0, one launch (start us, length us, event | category | flops | bytes accessed | tf_op | source)
XLA Modules:
  0.0 107.8 jit_solution(4943541214677913914)
XLA Ops:
  0.6 105.2 %shard_map.50 = (f32[2,256,1024]{2,1,0:T(8,128)S(1)}, f32[8,128]{1,0:T(8,128)}) custom-call(f32[2,256,1024]{2,1,0:T(8,128)} %rhs_in.1, f32[2,256,1024]{2,1,0:T(8,128)} %guess_in.1, f32[256,1024]{1,0:T(8,128)} %diff_in.1), custom_call_target="tpu_custom_call" | custom-call | tf_op jit(solution)/shard_map/pallas_call | solution.py:782
  105.8 0.0 copy-start
  105.8 1.3 %copy.6 = f32[2,256,1024]{2,1,0:T(8,128)} copy(f32[2,256,1024]{2,1,0:T(8,128)S(1)} %get-tuple-element.6) | data formatting | bytes 4194304
  107.2 0.0 copy-done
  107.2 0.6 slice_reduce_fusion
Async XLA Ops:
  105.8 1.3 %copy-start = (f32[8,128]{1,0:T(8,128)S(1)}, f32[8,128]{1,0:T(8,128)}, u32[]{:S(2)}) copy-start(f32[8,128]{1,0:T(8,128)} %get-tuple-element.5) | copy-start | bytes 12292
where the time goes:
time: 108 us
  Pallas kernels  105 us (97%)
  local copies, waits for them, and re-layouts  1.95 us (2%)
    pallas_call x1, Pallas kernels, fast_body(): pl.pallas_call(functools.partial(cycle_kernel, strips, devices, cells), o...  105 us

commit v1 on v0

--- a/solution.py
+++ b/solution.py
@@ -129,21 +129,21 @@
 def cycle_kernel(
     strips, devices, cells,
     rhs_in, guess_in, diff_in, out, norms_out,
-    rhs, guess, diff, v0, g1, v1, r1, v1f, sol, guess_e, v0_e, v1_e, v1f_e, sol_e,
-    pair, g2h, v2, c_g2, c_v2, c_g3, c_v3, c_g4, c_v4, c_v4b, finals, weights, tile, gathered, gathered_z,
-    load_sem, store_sem, zs_sem, zr_sem, ts_sem, tr_sem, ps_sem, pr_sem, as_sem, ar_sem, al_sem,
-    bs_sem, br_sem, bl_sem, rs_sem, credit, ns_sem, nr_sem, ms_sem, mr_sem,
+    rhs, guess, diff, v0, g1, v1f, sol, guess_e, v0_e, v1f_e, early, early_e, weights,
+    c_weights, c_sources, c_fields, c_finals, tile, gathered, gathered_z,
+    load_sem, store_sem, zs_sem, zr_sem, ts_sem, tr_sem, as_sem, ar_sem, al_sem,
+    bs_sem, br_sem, bl_sem, rs_sem, ns_sem, nr_sem, ms_sem, mr_sem,
 ):
     me = lax.axis_index("tm")
     strip = lax.axis_index("space")
     rows, width = rhs_in.shape[1], rhs_in.shape[2]
-    chips = devices // 2
     core = lax.rem(me, 2)
-    chip = me // 2
+    sibling = me + 1 - 2 * core
     low, high = EDGE, EDGE + rows
     first, last = me == 0, me == devices - 1
     top, bottom = strip == 0, strip == strips - 1
     piece = rows // devices
+    tall_piece = piece + 2 * TILE
 
     def aligned(value):
         return pl.multiple_of(value, TILE)
@@ -203,6 +203,12 @@
             rhs.at[:, before_low], rhs.at[:, after_high],
         ),
     ]
+    inside_halos = [
+        halo_pair(
+            3 + i, field.at[high - TILE:high], field.at[low:low + TILE], field.at[before_low], field.at[after_high],
+        )
+        for i, field in enumerate((g1, v1f, v1f_e))
+    ]
 
     def start_halo(pair_of):
         @pl.when(jnp.logical_not(bottom))
@@ -263,9 +269,7 @@
         guess_e, guess_parts,
     )
     v0_shift = shift(1, lambda start, size: v0.at[1, start:start + size], v0_e, whole)
-    v1_shift = shift(2, lambda start, size: v1.at[start:start + size], v1_e, whole)
-    v1f_shift = shift(3, lambda start, size: v1f.at[start:start + size], v1f_e, whole)
-    sol_shift = shift(4, lambda start, size: sol.at[1, start:start + size], sol_e, inner)
+    early_shift = shift(2, lambda start, size: early.at[start:start + size], early_e, inner)
     send(guess_shift[0])
     send(guess_shift[1])
 
@@ -293,13 +297,17 @@
         done = ahead + count * BLOCK
         return loop(start + done, (size - done) // TILE, TILE, carry)
 
+    def once(start, tall, step):
+        block[0] = tall
+        step(aligned(start), 0)
+        block[0] = TILE
+
     @pl.when(first)
     def _():
         def clear(r, carry):
             zero = jnp.zeros((block[0], width), jnp.float32)
-            for ref in (guess_e, v0_e, v1_e, v1f_e, sol_e):
+            for ref in (guess_e, v0_e, v1f_e, early_e):
                 ref[at(r), :] = zero
-            v2[1, at(r), :] = zero
             return carry
 
         blocks(low - TILE, rows + 2 * TILE, clear, 0, TILE)
@@ -309,12 +317,12 @@
         return blocks(start, size, step, init, TILE if j == 0 else 0)
 
     def clear_edge(start):
+        zero = jnp.zeros((TILE, width), jnp.float32)
         for ref in (guess, rhs):
             for p in range(2):
-                ref[p, start:start + TILE, :] = jnp.zeros((TILE, width), jnp.float32)
-        for p in range(2):
-            v2[p, start:start + TILE, :] = jnp.zeros((TILE, width), jnp.float32)
-        diff[start:start + TILE, :] = jnp.zeros((TILE, width), jnp.float32)
+                ref[p, start:start + TILE, :] = zero
+        for ref in (g1, v1f, v1f_e, diff):
+            ref[start:start + TILE, :] = zero
 
     @pl.when(top)
     def _():
@@ -337,16 +345,12 @@
     def tall_at(r):
         return pl.ds(aligned(r - TILE), block[0] + 2 * TILE)
 
-    def coefficients(level, r):
-        scaled = 2.0**level * diff[at(r), :]
-        diag = 1.0 + 4.0 * scaled
-        if level < 2:
-            return scaled, diag, weights[level, at(r), :]
-        return scaled, diag, damping / diag
+    def coefficients(r):
+        scaled = diff[at(r), :]
+        return scaled, 1.0 + 4.0 * scaled, weights[at(r), :]
 
     def set_weights(r, carry):
-        for level in range(2):
-            weights[level, at(r), :] = damping / (1.0 + 4.0 * (2.0**level * diff[at(r), :]))
+        weights[at(r), :] = damping / (1.0 + 4.0 * diff[at(r), :])
         return carry
 
     def squares(value, keep=None):
@@ -365,7 +369,7 @@
     keep_share = 1.0 - damping
 
     def sweep_last(r, carry):
-        scaled, _, weight = coefficients(0, r)
+        scaled, _, weight = coefficients(r)
         mid, total = stencil(guess[1, tall_at(r), :])
         v0[1, at(r), :] = keep_share * mid + weight * (rhs[1, at(r), :] + scaled * total + guess[0, at(r), :])
         return carry
@@ -375,7 +379,6 @@
     blocks(low, rows, set_weights)
     for j in (1, 2):
         chunk(j, sweep_last)
-        send(v0_shift[j])
     finish_halo(halos[0])
     send(guess_shift[2])
     send(guess_shift[3])
@@ -385,12 +388,33 @@
     blocks(high, TILE, set_weights)
     for j in (0, 3):
         chunk(j, sweep_last)
+    for j in (0, 3, 1, 2):
         send(v0_shift[j])
 
+    c_low, c_high = EDGE, EDGE + piece
+    c_rows = slice(c_low - TILE, c_high + TILE)
+    offset = me * piece
+
+    def coarse(step, init=0):
+        return blocks(c_low - TILE, tall_piece, step, init, TILE)
+
+    def coarse_diff(r):
+        return diff[at(aligned(r + offset)), :]
+
+    def set_coarse_weights(r, carry):
+        base = coarse_diff(r)
+        for level in range(1, LEVELS):
+            c_weights[level - 1, at(r), :] = damping / (1.0 + 4.0 * (2.0**level * base))
+        return carry
+
+    coarse(set_coarse_weights)
+
     def sweep_first(r, carry):
-        scaled, _, weight = coefficients(0, r)
+        scaled, _, weight = coefficients(r)
         mid, total = stencil(guess[0, tall_at(r), :])
-        v0[0, at(r), :] = keep_share * mid + weight * (rhs[0, at(r), :] + scaled * total + guess_e[at(r), :])
+        value = keep_share * mid + weight * (rhs[0, at(r), :] + scaled * total + guess_e[at(r), :])
+        v0[0, at(r), :] = value
+        early[at(r), :] = rhs[1, at(r), :] + value
         return carry
 
     for copy in guess_shift:
@@ -399,57 +423,24 @@
         chunk(j, sweep_first)
 
     def descend(r, carry):
-        keep = jnp.logical_and(r >= low, r < high)
-        scaled, diag, _ = coefficients(0, r)
+        scaled, diag, _ = coefficients(r)
         mid, total = stencil(v0[0, tall_at(r), :])
         one = rhs[0, at(r), :] - diag * mid + scaled * total + v0_e[at(r), :]
         late, total = stencil(v0[1, tall_at(r), :])
         two = rhs[1, at(r), :] - diag * late + scaled * total + mid
-        source = one + two
-        g1[at(r), :] = source
-        _, _, weight = coefficients(1, r)
-        v1[at(r), :] = weight * source
-        return carry + squares(one, keep) + squares(two, keep)
-
-    total0 = zero_tile
-    for j in range(4):
-        receive(v0_shift[j])
-        total0 = chunk(j, descend, total0)
-        send(v1_shift[j])
-
-    def residual1(r, carry):
-        keep = jnp.logical_and(r >= low, r < high)
-        scaled, _, _ = coefficients(1, r)
-        _, total = stencil(v1[tall_at(r), :])
-        resid = keep_share * g1[at(r), :] + scaled * total + v1_e[at(r), :]
-        r1[at(r), :] = resid
-        return carry + squares(resid, keep)
-
-    total1 = zero_tile
-    tall_piece = piece + 2 * TILE
-    c_low, c_high = EDGE, EDGE + piece
-    c_rows = slice(c_low - TILE, c_high + TILE)
-    sibling = me + 1 - 2 * core
-
-    def swap_of(k):
+        g1[at(r), :] = one + two
+        return carry + squares(one) + squares(two)
+
+    c_g1 = c_sources[0]
+
+    def hand_over(k):
         start = low - TILE + k * piece
-        return tm_copy(
-            r1.at[start:start + tall_piece], pair.at[k // 2], ps_sem.at[k // 2], pr_sem.at[k // 2], sibling
-        )
-
-    def hand_over(k):
-        return tm_copy(g2h.at[k // 2], c_g2.at[chip, c_rows], as_sem.at[k // 2], ar_sem.at[chip], k)
-
-    def join_piece(k):
-        start = low - TILE + k * piece
-
-        def join(r, carry):
-            g2h[k // 2, at(r), :] = r1[at(aligned(r + start)), :] + pair[k // 2, at(r), :]
-            return carry
-
-        swap_of(k).wait_recv()
-        blocks(0, tall_piece, join, 0, TILE)
-        local = pltpu.make_async_copy(g2h.at[k // 2], c_g2.at[chip, c_rows], al_sem)
+        source = g1.at[start:start + tall_piece]
+        return source, tm_copy(source, c_g1.at[me, c_rows], as_sem.at[k], ar_sem.at[me], k)
+
+    def give(k):
+        source, copy = hand_over(k)
+        local = pltpu.make_async_copy(source, c_g1.at[me, c_rows], al_sem)
 
         @pl.when(me == k)
         def _():
@@ -458,53 +449,59 @@
 
         @pl.when(me != k)
         def _():
-            hand_over(k).start()
-
-    done = 0
-    for j in range(4):
-        receive(v1_shift[j])
-        total1 = chunk(j, residual1, total1)
-        ready = (sum(whole[j]) - tall_piece - low + TILE) // piece + 1
-        for k in range(done, ready):
-            @pl.when(core != k % 2)
-            def _():
-                swap_of(k).start()
-        for k in range(done, ready):
-            @pl.when(core == k % 2)
-            def _():
-                join_piece(k)
-        done = ready
-    for c in range(chips):
-        copy = tm_copy(g2h.at[0], c_g2.at[c, c_rows], as_sem.at[0], ar_sem.at[c], sibling)
-
-        @pl.when(c != chip)
+            copy.start()
+
+    total0 = zero_tile
+    ready, given = [False] * 4, set()
+
+    def covered(k):
+        begin, end = max(0, k * piece - TILE), min(rows, (k + 1) * piece + TILE)
+        return all(ready[j] for j in range(4) if begin < (j + 1) * quarter and end > j * quarter)
+
+    edges = (0, devices - 1)
+    for j in (0, 3, 1, 2):
+        receive(v0_shift[j])
+        total0 = blocks(*inner[j], descend, total0)
+        ready[j] = True
+        if j == 3:
+            start_halo(inside_halos[0])
+        for k in range(devices):
+            if k not in given and k not in edges and covered(k):
+                given.add(k)
+                give(k)
+        if j == 1:
+            finish_halo(inside_halos[0])
+            for k in edges:
+                give(k)
+    send(early_shift[0])
+    send(early_shift[1])
+    for s in range(devices):
+        copy = tm_copy(c_g1.at[s, c_rows], c_g1.at[s, c_rows], as_sem.at[0], ar_sem.at[s], sibling)
+
+        @pl.when(s != me)
         def _():
             copy.wait_recv()
 
-    has_second = jnp.logical_and(core == 0, jnp.logical_not(first))
-
-    offset = me * piece
-
     def coarse_coefficients(level, r):
-        return coefficients(level, aligned(r + offset))
-
-
-    def coarse(step, init=0):
-        return blocks(c_low - TILE, tall_piece, step, init, TILE)
-
-    def first_sweep(level, source, field, count):
+        return 2.0**level * coarse_diff(r), c_weights[level - 1, at(r), :]
+
+    def first_sweep(level, count):
+        source, field = c_sources[level - 1], c_fields[level - 1]
+
         def step(r, carry):
-            _, _, weight = coarse_coefficients(level, r)
+            _, weight = coarse_coefficients(level, r)
             for p in range(count):
                 field[p, at(r), :] = weight * source[p, at(r), :]
             return carry
 
         coarse(step)
 
-    def coarse_residual(level, source, field, target, count):
+    def coarse_residual(level, count):
+        source, field, target = c_sources[level - 1], c_fields[level - 1], c_sources[level]
+
         def step(r, carry):
             keep = jnp.logical_and(r >= c_low, r < c_high)
-            scaled, _, _ = coarse_coefficients(level, r)
+            scaled, _ = coarse_coefficients(level, r)
             earlier, even = None, None
             for p in range(count):
                 mid, total = stencil(field[p, tall_at(r), :])
@@ -521,9 +518,12 @@
 
         return coarse(step, zero_tile)
 
-    def ascend(level, source, field, above, target, count):
+    def ascend(level, count):
+        source, field = c_sources[level - 1], c_fields[level - 1]
+        above, target = c_finals[level], c_finals[level - 1]
+
         def step(r, carry):
-            scaled, _, weight = coarse_coefficients(level, r)
+            scaled, weight = coarse_coefficients(level, r)
             earlier = None
             for p in range(count):
                 mid, total = stencil(field[p, tall_at(r), :] + above[p // 2, tall_at(r), :])
@@ -536,166 +536,148 @@
 
         coarse(step)
 
-    points2, points3 = chips, chips // 2
-    first_sweep(2, c_g2, c_v2, points2)
-    total2 = coarse_residual(2, c_g2, c_v2, c_g3, points2)
-    first_sweep(3, c_g3, c_v3, points3)
-    total3 = coarse_residual(3, c_g3, c_v3, c_g4, points3)
-    first_sweep(4, c_g4, c_v4, 1)
+    coarsest = LEVELS - 1
+    parts = [total0]
+    for level in range(1, coarsest):
+        first_sweep(level, devices >> (level - 1))
+        parts.append(coarse_residual(level, devices >> (level - 1)))
+    first_sweep(coarsest, 1)
+
+    source_l, field_l, final_l = c_sources[coarsest - 1], c_fields[coarsest - 1], c_finals[coarsest - 1]
 
     def second_sweep(r, carry):
-        scaled, _, weight = coarse_coefficients(4, r)
-        mid, total = stencil(c_v4[0, tall_at(r), :])
-        c_v4b[0, at(r), :] = keep_share * mid + weight * (c_g4[0, at(r), :] + scaled * total)
+        scaled, weight = coarse_coefficients(coarsest, r)
+        mid, total = stencil(field_l[0, tall_at(r), :])
+        final_l[0, at(r), :] = keep_share * mid + weight * (source_l[0, at(r), :] + scaled * total)
         return carry
 
     coarse(second_sweep)
-
-    def residual4(r, carry):
-        scaled, diag, _ = coarse_coefficients(4, r)
-        mid, total = stencil(c_v4b[0, tall_at(r), :])
-        return carry + squares(c_g4[0, at(r), :] - diag * mid + scaled * total)
-
-    total4 = blocks(c_low, piece, residual4, zero_tile)
-    c_v3f, c_v2f = finals
-    ascend(3, c_g3, c_v3, c_v4b, c_v3f, points3)
-    ascend(2, c_g2, c_v2, c_v3f, c_v2f, points2)
-
+    for level in range(coarsest - 1, 1, -1):
+        ascend(level, devices >> (level - 1))
+
+    c_v1, c_v2f, c_v1f = c_fields[0], c_finals[1], c_finals[0]
     back = []
     place = pl.ds(aligned(low + offset), piece)
-    for c in range(chips):
-        wants = [(0, 2 * c + core, c)]
-        if c > 0:
-            wants.append((1, 2 * c, c - 1))
-        for kind, target, point in wants:
-            src, dst = c_v2f.at[point, c_low:c_high], v2.at[kind, place]
-            copy = tm_copy(src, dst, bs_sem.at[kind, c], br_sem.at[kind, me], target)
-            local = pltpu.make_async_copy(src, dst, bl_sem.at[kind])
-            back.append((target, copy))
-
-            @pl.when(me == target)
-            def _():
-                local.start()
-                local.wait()
-
-            @pl.when(me != target)
-            def _():
-                copy.start()
-
-    relays = []
-    for i in range(chips):
-        for side in (core, 1 - core):
-            k = 2 * i + side
-            rows_of = pl.ds(aligned(low + k * piece), piece)
-            arrival = tm_copy(v2.at[0, rows_of], v2.at[0, rows_of], rs_sem.at[i], br_sem.at[0, k], sibling)
-            relays.append((k, arrival))
-    for k, arrival in relays[0::2]:
+
+    def give_back(kind, target, point, dst):
+        src = c_v1f.at[point, c_low:c_high]
+        copy = tm_copy(src, dst.at[place], bs_sem.at[kind, target], br_sem.at[kind, me], target)
+        local = pltpu.make_async_copy(src, dst.at[place], bl_sem.at[kind])
+        back.append((target, copy))
+
+        @pl.when(me == target)
+        def _():
+            local.start()
+            local.wait()
+
+        @pl.when(me != target)
+        def _():
+            copy.start()
+
+    block[0] = piece
+    scaled, weight = coarse_coefficients(1, c_low)
+    for p in range(devices):
+        mid, total = stencil(c_v1[p, tall_at(c_low), :] + c_v2f[p // 2, tall_at(c_low), :])
+        value = c_g1[p, at(c_low), :] + scaled * total
+        if p:
+            value = value + (c_v1[p - 1, at(c_low), :] + c_v2f[(p - 1) // 2, at(c_low), :])
+        c_v1f[p, at(c_low), :] = keep_share * mid + weight * value
+        give_back(0, p, p, v1f)
+    block[0] = TILE
+    for p in range(2, devices, 2):
+        give_back(1, p, p - 1, v1f_e)
+    send(early_shift[2])
+    send(early_shift[3])
+
+    def residual_l(r, carry):
+        scaled = 2.0**coarsest * coarse_diff(r)
+        mid, total = stencil(final_l[0, tall_at(r), :])
+        return carry + squares(source_l[0, at(r), :] - (1.0 + 4.0 * scaled) * mid + scaled * total)
+
+    parts.append(blocks(c_low, piece, residual_l, zero_tile))
+
+    order = [0, devices - 1] + list(range(1, devices - 1))
+
+    def rows_of(k):
+        return slice(low + k * piece, low + (k + 1) * piece)
+
+    def relay(k):
+        return tm_copy(v1f.at[rows_of(k)], v1f_e.at[rows_of(k)], rs_sem.at[k], br_sem.at[1, k], sibling)
+
+    for i, k in enumerate(order):
+        arrival = tm_copy(v1f.at[rows_of(k)], v1f.at[rows_of(k)], rs_sem.at[k], br_sem.at[0, k], sibling)
+
         @pl.when(k != me)
         def _():
             arrival.wait_recv()
 
-        arrival.start()
-    for k, arrival in relays[1::2]:
-        arrival.wait_recv()
-    for k in range(devices):
-        rows_of = slice(low + k * piece, low + (k + 1) * piece)
-        arrival = tm_copy(v2.at[1, rows_of], v2.at[1, rows_of], bs_sem.at[1, 0], br_sem.at[1, k], sibling)
-
-        @pl.when(jnp.logical_and(k != me, has_second))
-        def _():
-            arrival.wait_recv()
-
-    v2_halos = [
-        halo_pair(
-            3 + kind, v2.at[kind, high - TILE:high], v2.at[kind, low:low + TILE],
-            v2.at[kind, before_low], v2.at[kind, after_high],
-        )
-        for kind in range(2)
-    ]
-    start_halo(v2_halos[0])
-
-    @pl.when(has_second)
-    def _():
-        start_halo(v2_halos[1])
-
-    sends_on = jnp.logical_and(core == 1, jnp.logical_not(last))
-
-    @pl.when(has_second)
-    def _():
-        pl.semaphore_signal(credit, inc=1, device_id={"tm": me - 1, "space": strip}, device_id_type=DEVICE)
-
-    kind = 1 - core
-
-    def ascend1(r, carry):
-        scaled, _, weight = coefficients(1, r)
-        mid, total = stencil(v1[tall_at(r), :] + v2[0, tall_at(r), :])
-        earlier = v1_e[at(r), :] + v2[kind, at(r), :]
-        v1f[at(r), :] = keep_share * mid + weight * (g1[at(r), :] + scaled * total + earlier)
-        return carry
-
-    for j in (1, 2, 0, 3):
-        if j == 0:
-            finish_halo(v2_halos[0])
-
-            @pl.when(has_second)
-            def _():
-                finish_halo(v2_halos[1])
-
-        chunk(j, ascend1)
-        if j == 1:
-            @pl.when(sends_on)
-            def _():
-                pl.semaphore_wait(credit, 1)
-        send(v1f_shift[j])
+        @pl.when(core == 0)
+        def _():
+            relay(k).start()
+
+        if i == 1:
+            start_halo(inside_halos[1])
 
     def ascend_last(r, carry):
-        scaled, _, weight = coefficients(0, r)
+        scaled, _, weight = coefficients(r)
         mid, total = stencil(v0[1, tall_at(r), :] + v1f[tall_at(r), :])
         earlier = v0[0, at(r), :] + v1f[at(r), :]
         sol[1, at(r), :] = keep_share * mid + weight * (rhs[1, at(r), :] + scaled * total + earlier)
         return carry
 
-    blocks(low - TILE, TILE, ascend_last, 0)
-    for start, size in inner:
-        blocks(start, size, ascend_last, 0)
-    blocks(high, TILE, ascend_last, 0)
+    blocks(low + TILE, rows - 2 * TILE, ascend_last)
+    finish_halo(inside_halos[1])
+    once(low - TILE, 2 * TILE, ascend_last)
+    once(high - TILE, 2 * TILE, ascend_last)
+
+    for i, k in enumerate(order):
+        @pl.when(jnp.logical_and(jnp.logical_not(first), jnp.logical_or(core == 1, k != me)))
+        def _():
+            relay(k).wait_recv()
+
+        if i == 1:
+            @pl.when(jnp.logical_not(first))
+            def _():
+                start_halo(inside_halos[2])
 
     def ascend_first(r, carry):
-        scaled, _, weight = coefficients(0, r)
+        scaled, _, weight = coefficients(r)
         mid, total = stencil(v0[0, tall_at(r), :] + v1f[tall_at(r), :])
         earlier = v0_e[at(r), :] + v1f_e[at(r), :]
         sol[0, at(r), :] = keep_share * mid + weight * (rhs[0, at(r), :] + scaled * total + earlier)
         return carry
 
-    for j in range(4):
-        receive(v1f_shift[j])
-
-        @pl.when(jnp.logical_not(last))
-        def _():
-            v1f_shift[j].wait_send()
-            sol_shift[j].start()
-
-        chunk(j, ascend_first)
+    blocks(low + TILE, rows - 2 * TILE, ascend_first)
+
+    @pl.when(jnp.logical_not(first))
+    def _():
+        finish_halo(inside_halos[2])
+
+    once(low - TILE, 2 * TILE, ascend_first)
+    once(high - TILE, 2 * TILE, ascend_first)
     stores = pltpu.make_async_copy(sol.at[:, low:high], out, store_sem)
     stores.start()
 
     def final_last(r, carry):
-        scaled, diag, _ = coefficients(0, r)
+        scaled, diag, _ = coefficients(r)
         mid, total = stencil(sol[1, tall_at(r), :])
         return carry + squares(rhs[1, at(r), :] - diag * mid + scaled * total + sol[0, at(r), :])
 
     total5 = blocks(low, rows, final_last, zero_tile)
 
     def final_first(r, carry):
-        scaled, diag, _ = coefficients(0, r)
+        scaled, diag, weight = coefficients(r)
+        before = v1f_e[at(r), :]
+        mid, total = stencil(v0_e[tall_at(r), :] + v1f_e[tall_at(r), :])
+        sol_e = keep_share * mid + weight * (early_e[at(r), :] + scaled * total + before)
         mid, total = stencil(sol[0, tall_at(r), :])
-        return carry + squares(rhs[0, at(r), :] - diag * mid + scaled * total + sol_e[at(r), :])
-
-    for (start, size), arrived in zip(inner, sol_shift):
+        return carry + squares(rhs[0, at(r), :] - diag * mid + scaled * total + sol_e)
+
+    for (start, size), arrived in zip(inner, early_shift):
         receive(arrived)
         total5 = blocks(start, size, final_first, total5)
 
-    parts = [total0, total1, total2, total3, total4, total5]
+    parts.append(total5)
     for level, value in enumerate(parts):
         tile[level:level + 1, :] = jnp.sum(value, axis=0, keepdims=True)
     for level in range(len(parts), TILE):
@@ -726,21 +708,19 @@
     norms_out[...] = jnp.broadcast_to(jnp.sqrt(summed * (1.0 / cells)), (TILE, 128))
 
     stores.wait()
-    for group in (guess_shift, v0_shift, v1_shift, sol_shift):
+    for group in (guess_shift, v0_shift, early_shift):
         for copy in group:
             @pl.when(jnp.logical_not(last))
             def _():
                 copy.wait_send()
-    for _, copy in relays[0::2]:
-        copy.wait_send()
     for k in range(devices):
-        @pl.when(core != k % 2)
-        def _():
-            swap_of(k).wait_send()
-
-        @pl.when(jnp.logical_and(core == k % 2, me != k))
-        def _():
-            hand_over(k).wait_send()
+        @pl.when(me != k)
+        def _():
+            hand_over(k)[1].wait_send()
+
+        @pl.when(core == 0)
+        def _():
+            relay(k).wait_send()
     for target, copy in back:
         @pl.when(me != target)
         def _():
@@ -750,7 +730,6 @@
 def fast_body(rhs, guess, diffusion):
     devices, strips = lax.axis_size("tm"), lax.axis_size("space")
     rows, width = rhs.shape[1:]
-    chips = devices // 2
     cells = rows * strips * width
     height = rows + 2 * EDGE
     c_height = rows // devices + 2 * EDGE
@@ -761,21 +740,19 @@
     def coarse(count):
         return pltpu.VMEM((count, c_height, width), jnp.float32)
 
-    shared = pltpu.VMEM((chips, rows // devices + EDGE, width), jnp.float32)
+    def pyramid():
+        return tuple(coarse(devices >> level) for level in range(LEVELS - 1))
+
     dma = pltpu.SemaphoreType.DMA
     scratch = [
-        plane(2), plane(2), plane(), plane(2), plane(), plane(), plane(), plane(), plane(2),
-        plane(), plane(), plane(), plane(), plane(),
-        shared, shared, plane(2),
-        coarse(chips), coarse(chips), coarse(chips // 2), coarse(chips // 2), coarse(1), coarse(1), coarse(1),
-        (coarse(chips // 2), coarse(chips)),
-        plane(2),
+        plane(2), plane(2), plane(), plane(2), plane(), plane(), plane(2),
+        plane(), plane(), plane(), plane(), plane(), plane(),
+        coarse(LEVELS - 1), pyramid(), pyramid(), pyramid(),
         pltpu.VMEM((TILE, 128), jnp.float32),
         pltpu.VMEM((devices, TILE, 128), jnp.float32),
         pltpu.VMEM((strips, TILE, 128), jnp.float32),
-        dma((3,)), dma, dma((5, 2)), dma((5, 2)), dma((5, 4)), dma((5, 4)), dma((chips,)), dma((chips,)),
-        dma((chips,)), dma((chips,)), dma, dma((2, devices)), dma((2, devices)), dma((2,)),
-        dma((chips,)), pltpu.SemaphoreType.REGULAR,
+        dma((3,)), dma, dma((6, 2)), dma((6, 2)), dma((3, 4)), dma((3, 4)), dma((devices,)), dma((devices,)), dma,
+        dma((2, devices)), dma((2, devices)), dma((2,)), dma((devices,)),
         dma((devices,)), dma((devices,)), dma((strips,)), dma((strips,)),
     ]
     any_space = pl.BlockSpec(memory_space=pl.ANY)

time: 108 us -> 93.9 us (0.87)
  Pallas kernels: 105 us -> 91.1 us
    pallas_call x1, Pallas kernels: 105 us -> 91.1 us  [fast_body(): pl.pallas_call(functools.partial(cycle_kernel, strips, devices, cells), o...]
where the time goes in v1:
time: 93.9 us; the launch traced here: 93.7 us
  Pallas kernels  91.1 us (97%)
  local copies, waits for them, and re-layouts  1.95 us (2%)
    pallas_call x1, Pallas kernels, fast_body(): pl.pallas_call(functools.partial(cycle_kernel, strips, devices, cells), o...  91.1 us

profile of v1, /device:TPU:0, one launch (start us, length us, event | category | flops | bytes accessed | tf_op | source)
XLA Modules:
  0.0 93.7 jit_solution(6599356372740271935)
XLA Ops:
  0.6 91.1 %shard_map.50 = (f32[2,256,1024]{2,1,0:T(8,128)S(1)}, f32[8,128]{1,0:T(8,128)}) custom-call(f32[2,256,1024]{2,1,0:T(8,128)} %rhs_in.1, f32[2,256,1024]{2,1,0:T(8,128)} %guess_in.1, f32[256,1024]{1,0:T(8,128)} %diff_in.1), custom_call_target="tpu_custom_call" | custom-call | tf_op jit(solution)/shard_map/pallas_call | solution.py:759
  91.8 0.0 copy-start
  91.8 1.3 %copy.6 = f32[2,256,1024]{2,1,0:T(8,128)} copy(f32[2,256,1024]{2,1,0:T(8,128)S(1)} %get-tuple-element.6) | data formatting | bytes 4194304
  93.1 0.0 copy-done
  93.1 0.6 slice_reduce_fusion
Async XLA Ops:
  91.8 1.3 %copy-start = (f32[8,128]{1,0:T(8,128)S(1)}, f32[8,128]{1,0:T(8,128)}, u32[]{:S(2)}) copy-start(f32[8,128]{1,0:T(8,128)} %get-tuple-element.5) | copy-start | bytes 12292

commit v2 on v1

v2 whole, which is shorter than its diff:
```python
import functools

import jax
import jax.numpy as jnp
from jax import lax
from jax.experimental import pallas as pl
from jax.experimental.pallas import tpu as pltpu
from jax.sharding import PartitionSpec as P

LEVELS = 5


damping = 0.8


def with_halo(block, sides, width):
    for axis, dim in sides:
        count = lax.axis_size(axis)
        forward = [(i, i + 1) for i in range(count - 1)]
        backward = [(target, source) for source, target in forward]
        low = lax.ppermute(
            lax.slice_in_dim(block, block.shape[dim] - width, None, axis=dim), axis, forward
        )
        high = lax.ppermute(lax.slice_in_dim(block, 0, width, axis=dim), axis, backward)
        block = jnp.concatenate([low, block, high], axis=dim)
    return block


def shifted(value, axis, steps):
    count = lax.axis_size(axis)
    first, last = (max(0, -steps), min(count, count - steps))
    return lax.ppermute(value, axis, [(source, source + steps) for source in range(first, last)])


def from_partner(value, axis, apart):
    mask = 2**apart
    pairs = [(source, source ^ mask) for source in range(lax.axis_size(axis))]
    return lax.ppermute(value, axis, pairs)


def neighbours(field):
    rows = with_halo(field, (("space", 1),), 1)
    padded = jnp.pad(rows, ((0, 0), (0, 0), (1, 1)))
    total = padded[:, 2:, 1:-1] + padded[:, :-2, 1:-1]
    total = total + padded[:, 1:-1, 2:] + padded[:, 1:-1, :-2]
    return total


def residual(field, source, scaled, diag, stride):
    earlier = shifted(field[-1:], "tm", stride)
    before = jnp.concatenate([earlier, field[:-1]], axis=0)
    image = diag * field - scaled * neighbours(field) - before
    return source - image


def stride_of(level):
    if level == 0:
        return 1
    return 2 ** (level - 1)


def body(rhs, guess, diffusion):
    position = lax.axis_index("tm")
    cells = rhs.shape[1] * lax.axis_size("space") * rhs.shape[2]
    partials = []

    def weight_of(level):
        if level <= 1:
            return jnp.float32(1.0)
        stride = stride_of(level)
        return jnp.where(position % stride == stride - 1, 1.0, 0.0).astype(jnp.float32)

    def record(resid, level):
        local_part = jnp.sum(resid * resid) * weight_of(level)
        partials.append(local_part)

    sources = [rhs]
    fields = []
    field = guess
    for level in range(LEVELS - 1):
        source = sources[level]
        scaled = 2.0**level * diffusion
        diag = 1.0 + 4.0 * scaled
        stride = stride_of(level)
        if level == 0:
            field = field + damping * residual(field, source, scaled, diag, stride) / diag
        else:
            field = damping * source / diag
        resid = residual(field, source, scaled, diag, stride)
        record(resid, level)
        fields.append(field)
        if level == 0:
            coarse = resid[0:1] + resid[1:2]
        else:
            coarse = resid + from_partner(resid, "tm", level - 1)
        sources.append(coarse)
    level = LEVELS - 1
    source = sources[level]
    scaled = 2.0**level * diffusion
    diag = 1.0 + 4.0 * scaled
    stride = stride_of(level)
    field = damping * source / diag
    field = field + damping * residual(field, source, scaled, diag, stride) / diag
    resid = residual(field, source, scaled, diag, stride)
    record(resid, level)
    correction = field
    for level in range(LEVELS - 2, -1, -1):
        scaled = 2.0**level * diffusion
        diag = 1.0 + 4.0 * scaled
        stride = stride_of(level)
        field = fields[level] + correction
        field = field + damping * residual(field, sources[level], scaled, diag, stride) / diag
        correction = field
    scaled = 1.0 * diffusion
    diag = 1.0 + 4.0 * scaled
    resid = residual(correction, rhs, scaled, diag, 1)
    record(resid, 0)
    totals = lax.psum(jnp.stack(partials), ("tm", "space"))
    norms = jnp.sqrt(totals / cells)
    return (correction, norms)


DEVICE = pl.DeviceIdType.MESH
TILE = 8
EDGE = 2 * TILE
BLOCK = 64
EARLY = 2
LANES = 128


def cycle_kernel(
    strips, devices, cells,
    rhs_in, guess_in, diff_in, out, norms_out,
    rhs, guess, diff, v0, v1, v1f, sol, guess_e, v0_e, v1f_e, early, early_e, weights,
    c_weights, c_fields, c_sums, c_top, c_v1f, tile, gathered, gathered_z,
    load_sem, zs_sem, zr_sem, ts_sem, tr_sem, as_sem, ar_sem, al_sem,
    bs_sem, br_sem, bl_sem, rs_sem, ns_sem, nr_sem, ms_sem, mr_sem,
):
    me = lax.axis_index("tm")
    strip = lax.axis_index("space")
    rows, width = rhs_in.shape[1], rhs_in.shape[2]
    tiles = width // LANES
    core = lax.rem(me, 2)
    sibling = me + 1 - 2 * core
    low, high = EDGE, EDGE + rows
    first, last = me == 0, me == devices - 1
    top, bottom = strip == 0, strip == strips - 1
    piece = rows // devices
    tall_piece = piece + 2 * TILE

    def aligned(value):
        return pl.multiple_of(value, TILE)

    def tm_copy(src, dst, send, recv, target):
        return pltpu.make_async_remote_copy(
            src_ref=src, dst_ref=dst, send_sem=send, recv_sem=recv,
            device_id={"tm": target, "space": strip}, device_id_type=DEVICE,
        )

    def space_copy(src, dst, send, recv, target):
        return pltpu.make_async_remote_copy(
            src_ref=src, dst_ref=dst, send_sem=send, recv_sem=recv,
            device_id={"tm": me, "space": target}, device_id_type=DEVICE,
        )

    later = jnp.minimum(me + 1, devices - 1)
    inside = slice(low, high)

    def load(index, source, target):
        return [
            pltpu.make_async_copy(
                source.at[:, j * LANES:(j + 1) * LANES], target.at[j, inside], load_sem.at[index, j]
            )
            for j in range(tiles)
        ]

    loads = [
        load(0, guess_in.at[1], guess.at[1]), load(1, guess_in.at[0], guess.at[0]), load(2, diff_in, diff),
        load(3, rhs_in.at[1], rhs.at[1]), load(4, rhs_in.at[0], rhs.at[0]),
    ]
    for group in loads:
        for copy in group:
            copy.start()

    barrier = pltpu.get_barrier_semaphore()
    for i in range(1, devices):
        pl.semaphore_signal(
            barrier, inc=1, device_id={"tm": lax.rem(me + i, devices), "space": strip}, device_id_type=DEVICE
        )
    for i in range(1, strips):
        pl.semaphore_signal(
            barrier, inc=1, device_id={"tm": me, "space": lax.rem(strip + i, strips)}, device_id_type=DEVICE
        )

    def row_tiles(start, size):
        return [start + i * TILE for i in range(size // TILE)]

    def blocks(start, size, step, carry=0):
        count = size // BLOCK

        def run(i, carry):
            begin = aligned(start + i * BLOCK)
            for offset in range(0, BLOCK, TILE):
                carry = step(begin + offset, carry)
            return carry

        if count == 1:
            carry = run(0, carry)
        elif count:
            carry = lax.fori_loop(0, count, run, carry)
        for r in row_tiles(start + count * BLOCK, size - count * BLOCK):
            carry = step(r, carry)
        return carry

    def at(r):
        return pl.ds(r, TILE)

    zero = jnp.zeros((TILE, LANES), jnp.float32)

    @pl.when(first)
    def _():
        def clear(r, carry):
            for ref in (guess_e, v0_e, v1f_e, early_e):
                for j in range(tiles):
                    ref[j, at(r), :] = zero
            return carry

        blocks(low - TILE, rows + 2 * TILE, clear)

    def clear_edge(start):
        for j in range(tiles):
            for ref in (guess, rhs):
                for p in range(2):
                    ref[p, j, start:start + TILE, :] = zero
            for ref in (v1, v1f, v1f_e, diff):
                ref[j, start:start + TILE, :] = zero

    @pl.when(top)
    def _():
        clear_edge(low - TILE)

    @pl.when(bottom)
    def _():
        clear_edge(high)

    pl.semaphore_wait(barrier, devices + strips - 2)

    down = jnp.minimum(strip + 1, strips - 1)
    up = jnp.maximum(strip - 1, 0)

    def halo_pair(index, field, lead=()):
        def rows_at(start):
            return field.at[lead + (slice(None), slice(start, start + TILE))]

        return (
            space_copy(rows_at(high - TILE), rows_at(low - TILE), zs_sem.at[index, 0], zr_sem.at[index, 0], down),
            space_copy(rows_at(low), rows_at(high), zs_sem.at[index, 1], zr_sem.at[index, 1], up),
        )

    guess_halo = halo_pair(0, guess, (slice(None),))
    diff_halo = halo_pair(1, diff)
    rhs_halo = halo_pair(2, rhs, (slice(None),))
    v1_halo, v1f_halo, v1f_e_halo = [halo_pair(3 + i, field) for i, field in enumerate((v1, v1f, v1f_e))]

    def start_halo(pair_of):
        @pl.when(jnp.logical_not(bottom))
        def _():
            pair_of[0].start()

        @pl.when(jnp.logical_not(top))
        def _():
            pair_of[1].start()

    def finish_halo(pair_of):
        @pl.when(jnp.logical_not(top))
        def _():
            pair_of[0].wait_recv()
            pair_of[1].wait_send()

        @pl.when(jnp.logical_not(bottom))
        def _():
            pair_of[1].wait_recv()
            pair_of[0].wait_send()

    half = rows // 2
    quarter = rows // 4
    whole = [
        (low - TILE, quarter + TILE), (low + quarter, quarter),
        (low + 2 * quarter, quarter), (low + 3 * quarter, quarter + TILE),
    ]
    inner = [(low + quarter * j, quarter) for j in range(4)]
    guess_parts = [(low, half), (low + half, half), (low - TILE, TILE), (high, TILE)]

    def shift(stage, source, target, parts):
        return [
            tm_copy(
                source.at[:, start:start + size], target.at[:, start:start + size],
                ts_sem.at[stage, j], tr_sem.at[stage, j], later,
            )
            for j, (start, size) in enumerate(parts)
        ]

    def send(copy):
        @pl.when(jnp.logical_not(last))
        def _():
            copy.start()

    def receive(copy):
        @pl.when(jnp.logical_not(first))
        def _():
            copy.wait_recv()

    guess_shift = shift(0, guess.at[1], guess_e, guess_parts)
    v0_shift = shift(1, v0.at[1], v0_e, whole)
    early_shift = shift(2, early, early_e, inner)

    for copy in loads[0]:
        copy.wait()
    send(guess_shift[0])
    send(guess_shift[1])
    for copy in loads[1]:
        copy.wait()
    start_halo(guess_halo)
    for copy in loads[2]:
        copy.wait()
    start_halo(diff_halo)
    for copy in loads[3] + loads[4]:
        copy.wait()
    start_halo(rhs_halo)

    lane = lax.broadcasted_iota(jnp.int32, (TILE, LANES), 1)
    at_left, at_right = lane == 0, lane == LANES - 1

    def stencil(field, r):
        mids = [field[j, at(r), :] for j in range(tiles)]
        right = [zero] + [pltpu.roll(mid, 1, 1) for mid in mids]
        left = [pltpu.roll(mid, LANES - 1, 1) for mid in mids] + [zero]
        totals = []
        for j in range(tiles):
            total = field[j, at(r - 1), :] + field[j, at(r + 1), :]
            total = total + jnp.where(at_left, right[j], right[j + 1])
            totals.append(total + jnp.where(at_right, left[j + 1], left[j]))
        return mids, totals

    def squares(values):
        total = values[0] * values[0]
        for value in values[1:]:
            total = total + value * value
        return total

    keep_share = 1.0 - damping

    def set_weights(r, carry):
        for j in range(tiles):
            scaled = diff[j, at(r), :]
            for level in range(2):
                weights[level, j, at(r), :] = damping / (1.0 + 4.0 * (2.0**level * scaled))
        return carry

    def sweep(p, source, before, target, also=None):
        def step(r, carry):
            mids, totals = stencil(source, r)
            for j in range(tiles):
                inner_sum = rhs[p, j, at(r), :] + diff[j, at(r), :] * totals[j] + before[j, at(r), :]
                value = keep_share * mids[j] + weights[0, j, at(r), :] * inner_sum
                target[j, at(r), :] = value
                if also is not None:
                    also(j, r, value)
            return carry

        return step

    def level_residual(p, j, r, mid, total, before):
        scaled = diff[j, at(r), :]
        return rhs[p, j, at(r), :] - mid + scaled * (total - 4.0 * mid) + before

    sweep_last = sweep(1, guess.at[1], guess.at[0], v0.at[1])
    blocks(low, rows, set_weights)
    blocks(low + quarter, 2 * quarter, sweep_last)
    finish_halo(guess_halo)
    send(guess_shift[2])
    send(guess_shift[3])
    finish_halo(diff_halo)
    finish_halo(rhs_halo)
    set_weights(low - TILE, 0)
    set_weights(high, 0)
    for j in (0, 3):
        blocks(*whole[j], sweep_last)
    for j in (0, 3, 1, 2):
        send(v0_shift[j])

    c_low, c_high = EDGE, EDGE + piece
    c_rows = slice(c_low - TILE, c_high + TILE)
    c_tiles, c_own = row_tiles(c_low - TILE, tall_piece), row_tiles(c_low, piece)
    offset = me * piece

    def coarse_diff(j, r):
        return diff[j, at(aligned(r + offset)), :]

    def coarse_weights(i, carry):
        r = aligned(c_low - TILE + i * TILE)
        for j in range(tiles):
            base = coarse_diff(j, r)
            for level in range(1, LEVELS):
                c_weights[level - 1, j, at(r), :] = damping / (1.0 + 4.0 * (2.0**level * base))
        return carry

    lax.fori_loop(0, tall_piece // TILE, coarse_weights, 0)

    def keep_early(j, r, value):
        early[j, at(r), :] = rhs[1, j, at(r), :] + value

    for copy in guess_shift:
        receive(copy)
    blocks(low - TILE, rows + 2 * TILE, sweep(0, guess.at[0], guess_e, v0.at[0], keep_early))

    def descend(r, carry):
        firsts, totals = stencil(v0.at[0], r)
        lasts, totals_last = stencil(v0.at[1], r)
        ones, twos = [], []
        for j in range(tiles):
            ones.append(level_residual(0, j, r, firsts[j], totals[j], v0_e[j, at(r), :]))
            twos.append(level_residual(1, j, r, lasts[j], totals_last[j], firsts[j]))
            v1[j, at(r), :] = weights[1, j, at(r), :] * (ones[j] + twos[j])
        return carry + (squares(ones) + squares(twos))

    c_v1 = c_fields[0]

    def hand_over(k):
        start = low - TILE + k * piece
        source = v1.at[:, start:start + tall_piece]
        return source, tm_copy(source, c_v1.at[me, :, c_rows], as_sem.at[k], ar_sem.at[me], k)

    def give(k):
        source, copy = hand_over(k)
        local = pltpu.make_async_copy(source, c_v1.at[me, :, c_rows], al_sem)

        @pl.when(me == k)
        def _():
            local.start()
            local.wait()

        @pl.when(me != k)
        def _():
            copy.start()

    total0 = zero
    ready, given = [False] * 4, set()

    def covered(k):
        begin, end = max(0, k * piece - TILE), min(rows, (k + 1) * piece + TILE)
        return all(ready[j] for j in range(4) if begin < (j + 1) * quarter and end > j * quarter)

    edges = (0, devices - 1)
    for j in (0, 3, 1, 2):
        receive(v0_shift[j])
        total0 = blocks(*inner[j], descend, total0)
        ready[j] = True
        if j == 3:
            start_halo(v1_halo)
        for k in range(devices):
            if k not in given and k not in edges and covered(k):
                given.add(k)
                give(k)
        if j == 1:
            finish_halo(v1_halo)
            for k in edges:
                give(k)
    for copy in early_shift[:EARLY]:
        send(copy)
    for s in range(devices):
        copy = tm_copy(c_v1.at[s, :, c_rows], c_v1.at[s, :, c_rows], as_sem.at[0], ar_sem.at[s], sibling)

        @pl.when(s != me)
        def _():
            copy.wait_recv()

    coarsest = LEVELS - 1

    def coarse_residual(level):
        field, target = c_fields[level - 1], c_fields[level]
        count = devices >> (level - 1)
        carry = zero
        for r in c_tiles:
            own = c_low <= r < c_high
            scaled = [2.0**level * coarse_diff(j, r) for j in range(tiles)]
            earlier, even = None, None
            for p in range(count):
                mids, totals = stencil(field.at[p], r)
                resid = []
                for j in range(tiles):
                    value = 0.25 * mids[j] + scaled[j] * (mids[j] + totals[j])
                    resid.append(value + earlier[j] if p else value)
                earlier = mids
                if own:
                    carry = carry + squares(resid)
                if p % 2 == 0:
                    even = resid
                else:
                    for j in range(tiles):
                        target[p // 2, j, at(r), :] = c_weights[level, j, at(r), :] * (even[j] + resid[j])
        return carry

    def lift(level, p, j, r, value):
        for q in (2 * p, 2 * p + 1):
            c_sums[level - 1][q, j, at(r), :] = c_fields[level - 1][q, j, at(r), :] + value

    def coarse_final(level, p, r, mids, totals, scaled, earlier):
        values = []
        for j in range(tiles):
            value = scaled[j] * totals[j]
            if p:
                value = value + earlier[j]
            value = c_fields[level - 1][p, j, at(r), :] + c_weights[level - 1, j, at(r), :] * value
            values.append(keep_share * mids[j] + value)
        return values

    parts = [total0]
    for level in range(1, coarsest):
        parts.append(coarse_residual(level))

    field_l = c_fields[coarsest - 1].at[0]
    for r in c_tiles:
        mids, totals = stencil(field_l, r)
        for j in range(tiles):
            scaled = 2.0**coarsest * coarse_diff(j, r)
            value = (1.0 + keep_share) * mids[j] + c_weights[coarsest - 1, j, at(r), :] * (scaled * totals[j])
            c_top[j, at(r), :] = value
            lift(coarsest - 1, 0, j, r, value)
    for level in range(coarsest - 1, 1, -1):
        for r in c_tiles:
            scaled = [2.0**level * coarse_diff(j, r) for j in range(tiles)]
            earlier = None
            for p in range(devices >> (level - 1)):
                mids, totals = stencil(c_sums[level - 1].at[p], r)
                values = coarse_final(level, p, r, mids, totals, scaled, earlier)
                earlier = mids
                for j in range(tiles):
                    lift(level - 1, p, j, r, values[j])

    back = []
    place = pl.ds(aligned(low + offset), piece)

    def give_back(kind, target, point, field):
        src, dst = c_v1f.at[point, :, c_low:c_high], field.at[:, place]
        copy = tm_copy(src, dst, bs_sem.at[kind, target], br_sem.at[kind, me], target)
        local = pltpu.make_async_copy(src, dst, bl_sem.at[kind])
        back.append((target, copy))

        @pl.when(me == target)
        def _():
            local.start()
            local.wait()

        @pl.when(me != target)
        def _():
            copy.start()

    for part in range(0, devices, devices // 2):
        for r in c_own:
            scaled = [2.0 * coarse_diff(j, r) for j in range(tiles)]
            earlier = None
            if part:
                earlier = [c_sums[0][part - 1, j, at(r), :] for j in range(tiles)]
            for p in range(part, part + devices // 2):
                mids, totals = stencil(c_sums[0].at[p], r)
                values = coarse_final(1, p, r, mids, totals, scaled, earlier)
                earlier = mids
                for j in range(tiles):
                    c_v1f[p, j, at(r), :] = values[j]
        for p in range(part, part + devices // 2):
            give_back(0, p, p, v1f)
    for p in range(2, devices, 2):
        give_back(1, p, p - 1, v1f_e)
    for copy in early_shift[EARLY:]:
        send(copy)

    total_l = zero
    for r in c_own:
        mids, totals = stencil(c_top, r)
        resid = []
        for j in range(tiles):
            scaled = 2.0**coarsest * coarse_diff(j, r)
            ahead = (1.0 + keep_share / damping) * field_l[j, at(r), :] - mids[j]
            resid.append((1.0 + 4.0 * scaled) * ahead + scaled * totals[j])
        total_l = total_l + squares(resid)
    parts.append(total_l)

    @pl.when(jnp.logical_not(last))
    def _():
        for copy in v0_shift:
            copy.wait_send()

    order = [0, devices - 1] + list(range(1, devices - 1))

    def rows_of(k):
        return slice(low + k * piece, low + (k + 1) * piece)

    def relay(k):
        return tm_copy(v1f.at[:, rows_of(k)], v1f_e.at[:, rows_of(k)], rs_sem.at[k], br_sem.at[1, k], sibling)

    def absorb(fields, change, spots):
        for r in spots:
            for j in range(tiles):
                value = change[j, at(r), :]
                for field in fields:
                    field[j, at(r), :] = field[j, at(r), :] + value

    halo_tiles = (low - TILE, high)

    for i, k in enumerate(order):
        spots = v1f.at[:, rows_of(k)]
        arrival = tm_copy(spots, spots, rs_sem.at[k], br_sem.at[0, k], sibling)

        @pl.when(k != me)
        def _():
            arrival.wait_recv()

        @pl.when(core == 0)
        def _():
            relay(k).start()

        if i == 1:
            start_halo(v1f_halo)
        absorb((v0.at[0], v0.at[1]), v1f, row_tiles(low + k * piece, piece))

    def result(p):
        def store(j, r, value):
            out[p, at(r - low), j * LANES:(j + 1) * LANES] = value

        return store

    def ascend(p, before, finish):
        def final_sweep(store=None):
            return sweep(p, v0.at[p], before, sol.at[p], store)

        store = result(p)
        blocks(low + TILE, rows - 2 * TILE, final_sweep(store))
        finish()
        for r in halo_tiles:
            final_sweep()(r, 0)
        for r in (low, high - TILE):
            final_sweep(store)(r, 0)

    def finish_last():
        finish_halo(v1f_halo)
        absorb((v0.at[0], v0.at[1]), v1f, halo_tiles)

    ascend(1, v0.at[0], finish_last)

    for i, k in enumerate(order):
        @pl.when(jnp.logical_and(jnp.logical_not(first), jnp.logical_or(core == 1, k != me)))
        def _():
            relay(k).wait_recv()

        if i == 1:
            @pl.when(jnp.logical_not(first))
            def _():
                start_halo(v1f_e_halo)
        absorb((v0_e,), v1f_e, row_tiles(low + k * piece, piece))

    def finish_first():
        @pl.when(jnp.logical_not(first))
        def _():
            finish_halo(v1f_e_halo)

        absorb((v0_e,), v1f_e, halo_tiles)

    ascend(0, v0_e, finish_first)

    def final_last(r, carry):
        mids, totals = stencil(sol.at[1], r)
        return carry + squares([
            level_residual(1, j, r, mids[j], totals[j], sol[0, j, at(r), :]) for j in range(tiles)
        ])

    total5 = blocks(low, rows, final_last, zero)

    def final_first(r, carry):
        mids, totals = stencil(v0_e, r)
        befores = []
        for j in range(tiles):
            inner_sum = early_e[j, at(r), :] + v1f_e[j, at(r), :] + diff[j, at(r), :] * totals[j]
            befores.append(keep_share * mids[j] + weights[0, j, at(r), :] * inner_sum)
        mids, totals = stencil(sol.at[0], r)
        return carry + squares([
            level_residual(0, j, r, mids[j], totals[j], befores[j]) for j in range(tiles)
        ])

    for copy in early_shift:
        receive(copy)
    total5 = blocks(low, rows, final_first, total5)

    parts.append(total5)
    for level, value in enumerate(parts):
        tile[level:level + 1, :] = jnp.sum(value, axis=0, keepdims=True)
    for level in range(len(parts), TILE):
        tile[level:level + 1, :] = jnp.zeros((1, LANES), jnp.float32)

    def exchange(count, own, source, slots, copier, send_sems, recv_sems):
        slots[pl.ds(own, 1)] = source[...][None]
        sent = [
            copier(source, slots.at[own], send_sems.at[i], recv_sems.at[own], lax.rem(own + i, count))
            for i in range(1, count)
        ]
        for copy in sent:
            copy.start()
        for i in range(1, count):
            other = lax.rem(own + i, count)
            copier(source, slots.at[other], send_sems.at[i], recv_sems.at[other], other).wait_recv()
        for copy in sent:
            copy.wait_send()
        total = slots[0]
        for i in range(1, count):
            total = total + slots[i]
        return total

    total = exchange(devices, me, tile, gathered, tm_copy, ns_sem, nr_sem)
    tile[...] = total
    total = exchange(strips, strip, tile, gathered_z, space_copy, ms_sem, mr_sem)
    summed = jnp.sum(total, axis=1, keepdims=True)
    norms_out[...] = jnp.broadcast_to(jnp.sqrt(summed * (1.0 / cells)), (TILE, LANES))

    @pl.when(jnp.logical_not(last))
    def _():
        for copy in guess_shift + early_shift:
            copy.wait_send()

    for k in range(devices):
        @pl.when(me != k)
        def _():
            hand_over(k)[1].wait_send()

        @pl.when(core == 0)
        def _():
            relay(k).wait_send()
    for target, copy in back:
        @pl.when(me != target)
        def _():
            copy.wait_send()


def fast_body(rhs, guess, diffusion):
    devices, strips = lax.axis_size("tm"), lax.axis_size("space")
    rows, width = rhs.shape[1:]
    tiles = width // LANES
    cells = rows * strips * width

    def spread(height):
        return height + (TILE - height) % (4 * TILE)

    def plane(*lead):
        return pltpu.VMEM(lead + (tiles, spread(rows + 2 * EDGE), LANES), jnp.float32)

    def coarse(*lead):
        return pltpu.VMEM(lead + (tiles, spread(rows // devices + 2 * EDGE), LANES), jnp.float32)

    dma = pltpu.SemaphoreType.DMA
    scratch = [
        plane(2), plane(2), plane(), plane(2), plane(), plane(), plane(2),
        plane(), plane(), plane(), plane(), plane(), plane(2),
        coarse(LEVELS - 1), tuple(coarse(devices >> level) for level in range(LEVELS - 1)),
        tuple(coarse(devices >> level) for level in range(LEVELS - 2)), coarse(), coarse(devices),
        pltpu.VMEM((TILE, LANES), jnp.float32),
        pltpu.VMEM((devices, TILE, LANES), jnp.float32),
        pltpu.VMEM((strips, TILE, LANES), jnp.float32),
        dma((5, tiles)), dma((6, 2)), dma((6, 2)), dma((3, 4)), dma((3, 4)), dma((devices,)), dma((devices,)), dma,
        dma((2, devices)), dma((2, devices)), dma((2,)), dma((devices,)),
        dma((devices,)), dma((devices,)), dma((strips,)), dma((strips,)),
    ]
    any_space = pl.BlockSpec(memory_space=pl.ANY)
    result, norms = pl.pallas_call(
        functools.partial(cycle_kernel, strips, devices, cells),
        out_shape=(
            pltpu.VMEM(rhs.shape, jnp.float32),
            jax.ShapeDtypeStruct((TILE, LANES), jnp.float32),
        ),
        in_specs=[any_space] * 3,
        out_specs=(pl.BlockSpec(memory_space=pltpu.VMEM), pl.BlockSpec(memory_space=pltpu.VMEM)),
        scratch_shapes=scratch,
        compiler_params=pltpu.CompilerParams(
            collective_id=0, has_side_effects=True, vmem_limit_bytes=67_043_328 - rhs.size * 4 - 2**17
        ),
    )(rhs, guess, diffusion)
    return result, norms[:LEVELS + 1, 0]


def solution(mesh):
    in_specs = (P("tm", "space", None), P("tm", "space", None), P("space", None))
    out_specs = (P("tm", "space", None), P())

    def choose(rhs, guess, diffusion):
        points = rhs.shape[0] * lax.axis_size("tm")
        one_coarsest = points == 2 ** (LEVELS - 1) and rhs.shape[0] == 2
        even = rhs.shape[1] % (TILE * lax.axis_size("tm")) == 0 and rhs.shape[2] % 128 == 0
        if one_coarsest and even:
            return fast_body(rhs, guess, diffusion)
        return body(rhs, guess, diffusion)

    return jax.shard_map(choose, mesh=mesh, in_specs=in_specs, out_specs=out_specs, check_vma=False)
```

time: 93.9 us -> 93.6 us (level)
  no operation moved by 1% of the time
where the time goes in v2:
time: 93.6 us; the launch traced here: 93.5 us
  Pallas kernels  90.9 us (97%)
  local copies, waits for them, and re-layouts  1.95 us (2%)
    pallas_call x1, Pallas kernels, fast_body(): pl.pallas_call(functools.partial(cycle_kernel, strips, devices, cells), o...  90.9 us

profile of v2, /device:TPU:0, one launch (start us, length us, event | category | flops | bytes accessed | tf_op | source)
XLA Modules:
  0.0 93.5 jit_solution(15335505050902161525)
XLA Ops:
  0.6 90.9 %shard_map.50 = (f32[2,256,1024]{2,1,0:T(8,128)S(1)}, f32[8,128]{1,0:T(8,128)}) custom-call(f32[2,256,1024]{2,1,0:T(8,128)} %rhs_in.1, f32[2,256,1024]{2,1,0:T(8,128)} %guess_in.1, f32[256,1024]{1,0:T(8,128)} %diff_in.1), custom_call_target="tpu_custom_call" | custom-call | tf_op jit(solution)/shard_map/pallas_call | solution.py:772
  91.5 0.0 copy-start
  91.5 1.3 %copy.6 = f32[2,256,1024]{2,1,0:T(8,128)} copy(f32[2,256,1024]{2,1,0:T(8,128)S(1)} %get-tuple-element.6) | data formatting | bytes 4194304
  92.9 0.0 copy-done
  92.9 0.6 slice_reduce_fusion
Async XLA Ops:
  91.5 1.3 %copy-start = (f32[8,128]{1,0:T(8,128)S(1)}, f32[8,128]{1,0:T(8,128)}, u32[]{:S(2)}) copy-start(f32[8,128]{1,0:T(8,128)} %get-tuple-element.5) | copy-start | bytes 12292

commit v3 on v2

--- a/solution.py
+++ b/solution.py
@@ -124,7 +124,7 @@
 TILE = 8
 EDGE = 2 * TILE
 BLOCK = 64
-EARLY = 2
+EARLY = 3
 LANES = 128
 
 
@@ -142,6 +142,10 @@
     tiles = width // LANES
     core = lax.rem(me, 2)
     sibling = me + 1 - 2 * core
+    chip = me // 2
+    chip_x = chip + 1 - 2 * lax.rem(chip, 2)
+    chip_y = lax.rem(chip + 2, 4)
+    chip_xy = lax.rem(chip_x + 2, 4)
     low, high = EDGE, EDGE + rows
     first, last = me == 0, me == devices - 1
     top, bottom = strip == 0, strip == strips - 1
@@ -232,7 +236,7 @@
             for ref in (guess, rhs):
                 for p in range(2):
                     ref[p, j, start:start + TILE, :] = zero
-            for ref in (v1, v1f, v1f_e, diff):
+            for ref in (v1, v1f, guess_e, v0_e, diff):
                 ref[j, start:start + TILE, :] = zero
 
     @pl.when(top)
@@ -260,7 +264,9 @@
     guess_halo = halo_pair(0, guess, (slice(None),))
     diff_halo = halo_pair(1, diff)
     rhs_halo = halo_pair(2, rhs, (slice(None),))
-    v1_halo, v1f_halo, v1f_e_halo = [halo_pair(3 + i, field) for i, field in enumerate((v1, v1f, v1f_e))]
+    v1_halo, v1f_halo, guess_e_halo, v0_e_halo = [
+        halo_pair(3 + i, field) for i, field in enumerate((v1, v1f, guess_e, v0_e))
+    ]
 
     def start_halo(pair_of):
         @pl.when(jnp.logical_not(bottom))
@@ -289,7 +295,7 @@
         (low + 2 * quarter, quarter), (low + 3 * quarter, quarter + TILE),
     ]
     inner = [(low + quarter * j, quarter) for j in range(4)]
-    guess_parts = [(low, half), (low + half, half), (low - TILE, TILE), (high, TILE)]
+    guess_parts = [(low, half), (low + half, half)]
 
     def shift(stage, source, target, parts):
         return [
@@ -311,7 +317,7 @@
             copy.wait_recv()
 
     guess_shift = shift(0, guess.at[1], guess_e, guess_parts)
-    v0_shift = shift(1, v0.at[1], v0_e, whole)
+    v0_shift = shift(1, v0.at[1], v0_e, inner)
     early_shift = shift(2, early, early_e, inner)
 
     for copy in loads[0]:
@@ -378,8 +384,6 @@
     blocks(low, rows, set_weights)
     blocks(low + quarter, 2 * quarter, sweep_last)
     finish_halo(guess_halo)
-    send(guess_shift[2])
-    send(guess_shift[3])
     finish_halo(diff_halo)
     finish_halo(rhs_halo)
     set_weights(low - TILE, 0)
@@ -412,7 +416,21 @@
 
     for copy in guess_shift:
         receive(copy)
-    blocks(low - TILE, rows + 2 * TILE, sweep(0, guess.at[0], guess_e, v0.at[0], keep_early))
+
+    @pl.when(jnp.logical_not(first))
+    def _():
+        start_halo(guess_e_halo)
+
+    halo_tiles = (low - TILE, high)
+    sweep_first = sweep(0, guess.at[0], guess_e, v0.at[0], keep_early)
+    blocks(low, rows, sweep_first)
+
+    @pl.when(jnp.logical_not(first))
+    def _():
+        finish_halo(guess_e_halo)
+
+    for r in halo_tiles:
+        sweep_first(r, 0)
 
     def descend(r, carry):
         firsts, totals = stencil(v0.at[0], r)
@@ -426,46 +444,29 @@
 
     c_v1 = c_fields[0]
 
-    def hand_over(k):
-        start = low - TILE + k * piece
-        source = v1.at[:, start:start + tall_piece]
-        return source, tm_copy(source, c_v1.at[me, :, c_rows], as_sem.at[k], ar_sem.at[me], k)
-
-    def give(k):
-        source, copy = hand_over(k)
-        local = pltpu.make_async_copy(source, c_v1.at[me, :, c_rows], al_sem)
-
-        @pl.when(me == k)
-        def _():
-            local.start()
-            local.wait()
-
-        @pl.when(me != k)
-        def _():
-            copy.start()
+    def row_place(k, ahead=0):
+        return aligned(low - ahead + k * piece)
+
+    def hand_over(slot, k):
+        source = v1.at[:, pl.ds(row_place(k, TILE), tall_piece)]
+        return tm_copy(source, c_v1.at[me, :, c_rows], as_sem.at[slot], ar_sem.at[me], k)
 
     total0 = zero
-    ready, given = [False] * 4, set()
-
-    def covered(k):
-        begin, end = max(0, k * piece - TILE), min(rows, (k + 1) * piece + TILE)
-        return all(ready[j] for j in range(4) if begin < (j + 1) * quarter and end > j * quarter)
-
-    edges = (0, devices - 1)
     for j in (0, 3, 1, 2):
         receive(v0_shift[j])
         total0 = blocks(*inner[j], descend, total0)
-        ready[j] = True
         if j == 3:
             start_halo(v1_halo)
-        for k in range(devices):
-            if k not in given and k not in edges and covered(k):
-                given.add(k)
-                give(k)
-        if j == 1:
-            finish_halo(v1_halo)
-            for k in edges:
-                give(k)
+    finish_halo(v1_halo)
+    others = [2 * c + i for c in (chip_x, chip_y) for i in range(2)] + [sibling] + [2 * chip_xy, 2 * chip_xy + 1]
+    handed = [hand_over(slot, k) for slot, k in enumerate(others)]
+    for copy in handed:
+        copy.start()
+    local = pltpu.make_async_copy(
+        v1.at[:, pl.ds(row_place(me, TILE), tall_piece)], c_v1.at[me, :, c_rows], al_sem
+    )
+    local.start()
+    local.wait()
     for copy in early_shift[:EARLY]:
         send(copy)
     for s in range(devices):
@@ -539,39 +540,57 @@
                     lift(level - 1, p, j, r, values[j])
 
     back = []
-    place = pl.ds(aligned(low + offset), piece)
-
-    def give_back(kind, target, point, field):
-        src, dst = c_v1f.at[point, :, c_low:c_high], field.at[:, place]
-        copy = tm_copy(src, dst, bs_sem.at[kind, target], br_sem.at[kind, me], target)
+    place = pl.ds(row_place(me), piece)
+
+    def give_back(kind, slot, target, point):
+        src, dst = c_v1f.at[point, :, c_low:c_high], (v1f, v1f_e)[kind].at[:, place]
+        return tm_copy(src, dst, bs_sem.at[kind, slot], br_sem.at[kind, me], target)
+
+    def keep_back(kind, point):
+        src, dst = c_v1f.at[point, :, c_low:c_high], (v1f, v1f_e)[kind].at[:, place]
         local = pltpu.make_async_copy(src, dst, bl_sem.at[kind])
-        back.append((target, copy))
-
-        @pl.when(me == target)
-        def _():
-            local.start()
-            local.wait()
-
-        @pl.when(me != target)
-        def _():
-            copy.start()
-
-    for part in range(0, devices, devices // 2):
-        for r in c_own:
-            scaled = [2.0 * coarse_diff(j, r) for j in range(tiles)]
-            earlier = None
-            if part:
-                earlier = [c_sums[0][part - 1, j, at(r), :] for j in range(tiles)]
-            for p in range(part, part + devices // 2):
-                mids, totals = stencil(c_sums[0].at[p], r)
-                values = coarse_final(1, p, r, mids, totals, scaled, earlier)
-                earlier = mids
-                for j in range(tiles):
-                    c_v1f[p, j, at(r), :] = values[j]
-        for p in range(part, part + devices // 2):
-            give_back(0, p, p, v1f)
-    for p in range(2, devices, 2):
-        give_back(1, p, p - 1, v1f_e)
+        local.start()
+        local.wait()
+
+    for r in c_own:
+        scaled = [2.0 * coarse_diff(j, r) for j in range(tiles)]
+        earlier = None
+        for p in range(devices):
+            mids, totals = stencil(c_sums[0].at[p], r)
+            values = coarse_final(1, p, r, mids, totals, scaled, earlier)
+            earlier = mids
+            for j in range(tiles):
+                c_v1f[p, j, at(r), :] = values[j]
+    back_own = [give_back(0, slot, k, k) for slot, k in enumerate(others)]
+    back_before = [give_back(1, slot, 2 * c, jnp.maximum(2 * c - 1, 0)) for slot, c in enumerate((chip_x, chip_y, chip_xy))]
+    to_sibling = give_back(1, 3, sibling, jnp.maximum(sibling - 1, 0))
+    has_before = [c > 0 for c in (chip_x, chip_y, chip_xy)]
+    inner_chip = jnp.logical_and(core == 1, chip > 0)
+
+    def start_before(i):
+        @pl.when(has_before[i])
+        def _():
+            back_before[i].start()
+
+    for copy in back_own[:4]:
+        copy.start()
+    start_before(0)
+    start_before(1)
+    for copy in back_own[5:]:
+        copy.start()
+    start_before(2)
+    back_own[4].start()
+
+    @pl.when(inner_chip)
+    def _():
+        to_sibling.start()
+
+    keep_back(0, me)
+
+    @pl.when(jnp.logical_and(core == 0, chip > 0))
+    def _():
+        keep_back(1, jnp.maximum(me - 1, 0))
+
     for copy in early_shift[EARLY:]:
         send(copy)
 
@@ -591,90 +610,94 @@
         for copy in v0_shift:
             copy.wait_send()
 
-    order = [0, devices - 1] + list(range(1, devices - 1))
-
-    def rows_of(k):
-        return slice(low + k * piece, low + (k + 1) * piece)
-
-    def relay(k):
-        return tm_copy(v1f.at[:, rows_of(k)], v1f_e.at[:, rows_of(k)], rs_sem.at[k], br_sem.at[1, k], sibling)
-
-    def absorb(fields, change, spots):
+    def spots_of(field, k):
+        return field.at[:, pl.ds(row_place(k), piece)]
+
+    def relay(slot, k):
+        return tm_copy(spots_of(v1f, k), spots_of(v1f_e, k), rs_sem.at[slot], br_sem.at[1, k], sibling)
+
+    def absorb(spots):
         for r in spots:
             for j in range(tiles):
-                value = change[j, at(r), :]
-                for field in fields:
-                    field[j, at(r), :] = field[j, at(r), :] + value
-
-    halo_tiles = (low - TILE, high)
-
-    for i, k in enumerate(order):
-        spots = v1f.at[:, rows_of(k)]
-        arrival = tm_copy(spots, spots, rs_sem.at[k], br_sem.at[0, k], sibling)
-
-        @pl.when(k != me)
-        def _():
-            arrival.wait_recv()
+                value = v1f[j, at(r), :]
+                for p in range(2):
+                    v0[p, j, at(r), :] = v0[p, j, at(r), :] + value
+
+    order = [me, sibling] + others[:4] + others[5:]
+    relays = [relay(slot, k) for slot, k in enumerate(order)]
+
+    def place_tiles(k):
+        return [row_place(k) + i * TILE for i in range(piece // TILE)]
+
+    for slot, k in enumerate(order):
+        if slot:
+            spots = spots_of(v1f, k)
+            tm_copy(spots, spots, rs_sem.at[slot], br_sem.at[0, k], sibling).wait_recv()
 
         @pl.when(core == 0)
         def _():
-            relay(k).start()
-
-        if i == 1:
-            start_halo(v1f_halo)
-        absorb((v0.at[0], v0.at[1]), v1f, row_tiles(low + k * piece, piece))
-
-    def result(p):
-        def store(j, r, value):
-            out[p, at(r - low), j * LANES:(j + 1) * LANES] = value
-
-        return store
-
-    def ascend(p, before, finish):
-        def final_sweep(store=None):
-            return sweep(p, v0.at[p], before, sol.at[p], store)
-
-        store = result(p)
-        blocks(low + TILE, rows - 2 * TILE, final_sweep(store))
-        finish()
-        for r in halo_tiles:
-            final_sweep()(r, 0)
-        for r in (low, high - TILE):
-            final_sweep(store)(r, 0)
-
-    def finish_last():
-        finish_halo(v1f_halo)
-        absorb((v0.at[0], v0.at[1]), v1f, halo_tiles)
-
-    ascend(1, v0.at[0], finish_last)
-
-    for i, k in enumerate(order):
-        @pl.when(jnp.logical_and(jnp.logical_not(first), jnp.logical_or(core == 1, k != me)))
-        def _():
-            relay(k).wait_recv()
-
-        if i == 1:
-            @pl.when(jnp.logical_not(first))
-            def _():
-                start_halo(v1f_e_halo)
-        absorb((v0_e,), v1f_e, row_tiles(low + k * piece, piece))
-
-    def finish_first():
-        @pl.when(jnp.logical_not(first))
-        def _():
-            finish_halo(v1f_e_halo)
-
-        absorb((v0_e,), v1f_e, halo_tiles)
-
-    ascend(0, v0_e, finish_first)
+            relays[slot].start()
+
+        absorb(place_tiles(k))
+    start_halo(v1f_halo)
+
+    def ascend_last(r, carry, store=True):
+        mids, totals = stencil(v0.at[1], r)
+        for j in range(tiles):
+            inner_sum = rhs[1, j, at(r), :] + diff[j, at(r), :] * totals[j] + v0[0, j, at(r), :]
+            value = keep_share * mids[j] + weights[0, j, at(r), :] * inner_sum
+            sol[1, j, at(r), :] = value
+            if store:
+                out[1, at(r - low), j * LANES:(j + 1) * LANES] = value
+        return carry
+
+    def ascend_first(r, carry):
+        mids, totals = stencil(v0.at[0], r)
+        for j in range(tiles):
+            inner_sum = rhs[0, j, at(r), :] + diff[j, at(r), :] * totals[j]
+            sol[0, j, at(r), :] = keep_share * mids[j] + weights[0, j, at(r), :] * inner_sum
+        return carry
+
+    blocks(low + TILE, rows - 2 * TILE, ascend_last)
+    finish_halo(v1f_halo)
+    absorb(halo_tiles)
+    for r in (low, high - TILE):
+        ascend_last(r, 0)
+    for r in halo_tiles:
+        ascend_last(r, 0, False)
+    blocks(low - TILE, rows + 2 * TILE, ascend_first)
 
     def final_last(r, carry):
         mids, totals = stencil(sol.at[1], r)
-        return carry + squares([
-            level_residual(1, j, r, mids[j], totals[j], sol[0, j, at(r), :]) for j in range(tiles)
-        ])
-
-    total5 = blocks(low, rows, final_last, zero)
+        for j in range(tiles):
+            rhs[1, j, at(r), :] = level_residual(1, j, r, mids[j], totals[j], 0.0)
+        return carry
+
+    blocks(low, rows, final_last)
+
+    def complete(r, carry):
+        resid = []
+        for j in range(tiles):
+            before = v0_e[j, at(r), :] + v1f_e[j, at(r), :]
+            v0_e[j, at(r), :] = before
+            value = sol[0, j, at(r), :] + weights[0, j, at(r), :] * before
+            sol[0, j, at(r), :] = value
+            out[0, at(r - low), j * LANES:(j + 1) * LANES] = value
+            resid.append(rhs[1, j, at(r), :] + value)
+        return carry + squares(resid)
+
+    total5 = zero
+    for slot, k in enumerate(order):
+        @pl.when(jnp.logical_or(core == 1, chip > 0) if slot else core == 1)
+        def _():
+            relays[slot].wait_recv()
+
+        for r in place_tiles(k):
+            total5 = complete(r, total5)
+
+    @pl.when(jnp.logical_not(first))
+    def _():
+        start_halo(v0_e_halo)
 
     def final_first(r, carry):
         mids, totals = stencil(v0_e, r)
@@ -689,7 +712,17 @@
 
     for copy in early_shift:
         receive(copy)
-    total5 = blocks(low, rows, final_first, total5)
+    total5 = blocks(low + TILE, rows - 2 * TILE, final_first, total5)
+
+    @pl.when(jnp.logical_not(first))
+    def _():
+        finish_halo(v0_e_halo)
+
+    for r in halo_tiles:
+        for j in range(tiles):
+            sol[0, j, at(r), :] = sol[0, j, at(r), :] + weights[0, j, at(r), :] * v0_e[j, at(r), :]
+    for r in (low, high - TILE):
+        total5 = final_first(r, total5)
 
     parts.append(total5)
     for level, value in enumerate(parts):
@@ -726,17 +759,20 @@
         for copy in guess_shift + early_shift:
             copy.wait_send()
 
-    for k in range(devices):
-        @pl.when(me != k)
-        def _():
-            hand_over(k)[1].wait_send()
-
-        @pl.when(core == 0)
-        def _():
-            relay(k).wait_send()
-    for target, copy in back:
-        @pl.when(me != target)
-        def _():
+    for copy in handed + back_own:
+        copy.wait_send()
+    for i in range(3):
+        @pl.when(has_before[i])
+        def _():
+            back_before[i].wait_send()
+
+    @pl.when(inner_chip)
+    def _():
+        to_sibling.wait_send()
+
+    @pl.when(core == 0)
+    def _():
+        for copy in relays:
             copy.wait_send()
 
 
@@ -764,7 +800,7 @@
         pltpu.VMEM((TILE, LANES), jnp.float32),
         pltpu.VMEM((devices, TILE, LANES), jnp.float32),
         pltpu.VMEM((strips, TILE, LANES), jnp.float32),
-        dma((5, tiles)), dma((6, 2)), dma((6, 2)), dma((3, 4)), dma((3, 4)), dma((devices,)), dma((devices,)), dma,
+        dma((5, tiles)), dma((7, 2)), dma((7, 2)), dma((3, 4)), dma((3, 4)), dma((devices,)), dma((devices,)), dma,
         dma((2, devices)), dma((2, devices)), dma((2,)), dma((devices,)),
         dma((devices,)), dma((devices,)), dma((strips,)), dma((strips,)),
     ]

time: 93.6 us -> 91.9 us (0.982)
  Pallas kernels: 90.9 us -> 89.1 us
    pallas_call x1, Pallas kernels: 90.9 us -> 89.1 us  [fast_body(): pl.pallas_call(functools.partial(cycle_kernel, strips, devices, cells), o...]
where the time goes in v3:
time: 91.9 us; the launch traced here: 91.7 us
  Pallas kernels  89.1 us (97%)
  local copies, waits for them, and re-layouts  1.95 us (2%)
    pallas_call x1, Pallas kernels, fast_body(): pl.pallas_call(functools.partial(cycle_kernel, strips, devices, cells), o...  89.1 us

profile of v3, /device:TPU:0, one launch (start us, length us, event | category | flops | bytes accessed | tf_op | source)
XLA Modules:
  0.0 91.7 jit_solution(7694047496491195877)
XLA Ops:
  0.6 89.1 %shard_map.50 = (f32[2,256,1024]{2,1,0:T(8,128)S(1)}, f32[8,128]{1,0:T(8,128)}) custom-call(f32[2,256,1024]{2,1,0:T(8,128)} %rhs_in.1, f32[2,256,1024]{2,1,0:T(8,128)} %guess_in.1, f32[256,1024]{1,0:T(8,128)} %diff_in.1), custom_call_target="tpu_custom_call" | custom-call | tf_op jit(solution)/shard_map/pallas_call | solution.py:808
  89.8 0.0 copy-start
  89.8 1.3 %copy.6 = f32[2,256,1024]{2,1,0:T(8,128)} copy(f32[2,256,1024]{2,1,0:T(8,128)S(1)} %get-tuple-element.6) | data formatting | bytes 4194304
  91.1 0.0 copy-done
  91.1 0.6 slice_reduce_fusion
Async XLA Ops:
  89.8 1.3 %copy-start = (f32[8,128]{1,0:T(8,128)S(1)}, f32[8,128]{1,0:T(8,128)}, u32[]{:S(2)}) copy-start(f32[8,128]{1,0:T(8,128)} %get-tuple-element.5) | copy-start | bytes 12292

commit v4 on v3

--- a/solution.py
+++ b/solution.py
@@ -124,7 +124,7 @@
 TILE = 8
 EDGE = 2 * TILE
 BLOCK = 64
-EARLY = 3
+EARLY = 2
 LANES = 128
 
 
@@ -132,9 +132,9 @@
     strips, devices, cells,
     rhs_in, guess_in, diff_in, out, norms_out,
     rhs, guess, diff, v0, v1, v1f, sol, guess_e, v0_e, v1f_e, early, early_e, weights,
-    c_weights, c_fields, c_sums, c_top, c_v1f, tile, gathered, gathered_z,
+    c_weights, c_fields, c_sums, c_top, c_v1f, tile, gathered, gathered_z, final_row, final_rows,
     load_sem, zs_sem, zr_sem, ts_sem, tr_sem, as_sem, ar_sem, al_sem,
-    bs_sem, br_sem, bl_sem, rs_sem, ns_sem, nr_sem, ms_sem, mr_sem,
+    hs_sem, hr_sem, bs_sem, br_sem, bl_sem, rs_sem, ns_sem, nr_sem, ms_sem, mr_sem, fs_sem, fr_sem,
 ):
     me = lax.axis_index("tm")
     strip = lax.axis_index("space")
@@ -191,10 +191,12 @@
         pl.semaphore_signal(
             barrier, inc=1, device_id={"tm": lax.rem(me + i, devices), "space": strip}, device_id_type=DEVICE
         )
-    for i in range(1, strips):
-        pl.semaphore_signal(
-            barrier, inc=1, device_id={"tm": me, "space": lax.rem(strip + i, strips)}, device_id_type=DEVICE
-        )
+    down = jnp.minimum(strip + 1, strips - 1)
+    up = jnp.maximum(strip - 1, 0)
+    for edge, beside in ((top, up), (bottom, down)):
+        @pl.when(jnp.logical_not(edge))
+        def _():
+            pl.semaphore_signal(barrier, inc=1, device_id={"tm": me, "space": beside}, device_id_type=DEVICE)
 
     def row_tiles(start, size):
         return [start + i * TILE for i in range(size // TILE)]
@@ -247,10 +249,7 @@
     def _():
         clear_edge(high)
 
-    pl.semaphore_wait(barrier, devices + strips - 2)
-
-    down = jnp.minimum(strip + 1, strips - 1)
-    up = jnp.maximum(strip - 1, 0)
+    pl.semaphore_wait(barrier, devices + 1 - top.astype(jnp.int32) - bottom.astype(jnp.int32))
 
     def halo_pair(index, field, lead=()):
         def rows_at(start):
@@ -447,9 +446,13 @@
     def row_place(k, ahead=0):
         return aligned(low - ahead + k * piece)
 
-    def hand_over(slot, k):
-        source = v1.at[:, pl.ds(row_place(k, TILE), tall_piece)]
-        return tm_copy(source, c_v1.at[me, :, c_rows], as_sem.at[slot], ar_sem.at[me], k)
+    def hand_over(slot, k, side):
+        ahead, size = TILE * (1 - side), piece + TILE
+        return tm_copy(
+            v1.at[:, pl.ds(row_place(k, ahead), size)],
+            c_v1.at[me, :, pl.ds(aligned(c_low - ahead), size)],
+            as_sem.at[slot], ar_sem.at[me], k,
+        )
 
     total0 = zero
     for j in (0, 3, 1, 2):
@@ -459,22 +462,33 @@
             start_halo(v1_halo)
     finish_halo(v1_halo)
     others = [2 * c + i for c in (chip_x, chip_y) for i in range(2)] + [sibling] + [2 * chip_xy, 2 * chip_xy + 1]
-    handed = [hand_over(slot, k) for slot, k in enumerate(others)]
+    far = others[:4] + others[5:]
+    tall_here = v1.at[:, pl.ds(row_place(me, TILE), tall_piece)]
+    tall_there = v1.at[:, pl.ds(row_place(sibling, TILE), tall_piece)]
+    handed = [hand_over(slot, k, slot % 2) for slot, k in enumerate(far)]
+    handed.insert(4, tm_copy(tall_there, c_v1.at[me, :, c_rows], as_sem.at[6], ar_sem.at[me], sibling))
     for copy in handed:
         copy.start()
-    local = pltpu.make_async_copy(
-        v1.at[:, pl.ds(row_place(me, TILE), tall_piece)], c_v1.at[me, :, c_rows], al_sem
-    )
+    local = pltpu.make_async_copy(tall_here, c_v1.at[me, :, c_rows], al_sem)
     local.start()
     local.wait()
     for copy in early_shift[:EARLY]:
         send(copy)
-    for s in range(devices):
-        copy = tm_copy(c_v1.at[s, :, c_rows], c_v1.at[s, :, c_rows], as_sem.at[0], ar_sem.at[s], sibling)
-
-        @pl.when(s != me)
-        def _():
-            copy.wait_recv()
+    mine = pl.ds(aligned(c_low - TILE * (1 - core)), piece + TILE)
+    inner_edge = pl.ds(aligned(c_low + (1 - core) * (piece - TILE)), TILE)
+    outer_edge = pl.ds(aligned(c_low - TILE + core * (piece + TILE)), TILE)
+    swaps = [
+        tm_copy(c_v1.at[k, :, inner_edge], c_v1.at[k, :, outer_edge], hs_sem.at[slot], hr_sem.at[k], sibling)
+        for slot, k in enumerate(far)
+    ]
+    for swap, k in zip(swaps, far):
+        spot = c_v1.at[k, :, mine]
+        tm_copy(spot, spot, hs_sem.at[0], ar_sem.at[k], sibling).wait_recv()
+        swap.start()
+    spot = c_v1.at[sibling, :, c_rows]
+    tm_copy(spot, spot, hs_sem.at[0], ar_sem.at[sibling], sibling).wait_recv()
+    for swap in swaps:
+        swap.wait_recv()
 
     coarsest = LEVELS - 1
 
@@ -539,7 +553,44 @@
                 for j in range(tiles):
                     lift(level - 1, p, j, r, values[j])
 
-    back = []
+    total_l = zero
+    for r in c_own:
+        mids, totals = stencil(c_top, r)
+        resid = []
+        for j in range(tiles):
+            scaled = 2.0**coarsest * coarse_diff(j, r)
+            ahead = (1.0 + keep_share / damping) * field_l[j, at(r), :] - mids[j]
+            resid.append((1.0 + 4.0 * scaled) * ahead + scaled * totals[j])
+        total_l = total_l + squares(resid)
+    parts.append(total_l)
+    tile[...] = jnp.zeros((TILE, LANES), jnp.float32)
+    for level, value in enumerate(parts):
+        tile[level:level + 1, :] = jnp.sum(value, axis=0, keepdims=True)
+
+    def begin_sum(count, own, slots, copier, send_sems, recv_sems):
+        slots[pl.ds(own, 1)] = tile[...][None]
+        sent = [
+            copier(tile, slots.at[own], send_sems.at[i], recv_sems.at[own], lax.rem(own + i, count))
+            for i in range(1, count)
+        ]
+        for copy in sent:
+            copy.start()
+
+        def end_sum():
+            for i in range(1, count):
+                other = lax.rem(own + i, count)
+                copier(tile, slots.at[other], send_sems.at[i], recv_sems.at[other], other).wait_recv()
+            for copy in sent:
+                copy.wait_send()
+            total = slots[0]
+            for i in range(1, count):
+                total = total + slots[i]
+            tile[...] = total
+
+        return end_sum
+
+    end_time_sum = begin_sum(devices, me, gathered, tm_copy, ns_sem, nr_sem)
+
     place = pl.ds(row_place(me), piece)
 
     def give_back(kind, slot, target, point):
@@ -594,17 +645,6 @@
     for copy in early_shift[EARLY:]:
         send(copy)
 
-    total_l = zero
-    for r in c_own:
-        mids, totals = stencil(c_top, r)
-        resid = []
-        for j in range(tiles):
-            scaled = 2.0**coarsest * coarse_diff(j, r)
-            ahead = (1.0 + keep_share / damping) * field_l[j, at(r), :] - mids[j]
-            resid.append((1.0 + 4.0 * scaled) * ahead + scaled * totals[j])
-        total_l = total_l + squares(resid)
-    parts.append(total_l)
-
     @pl.when(jnp.logical_not(last))
     def _():
         for copy in v0_shift:
@@ -640,6 +680,8 @@
 
         absorb(place_tiles(k))
     start_halo(v1f_halo)
+    end_time_sum()
+    end_strip_sum = begin_sum(strips, strip, gathered_z, space_copy, ms_sem, mr_sem)
 
     def ascend_last(r, carry, store=True):
         mids, totals = stencil(v0.at[1], r)
@@ -674,7 +716,6 @@
         return carry
 
     blocks(low, rows, final_last)
-
     def complete(r, carry):
         resid = []
         for j in range(tiles):
@@ -710,9 +751,11 @@
             level_residual(0, j, r, mids[j], totals[j], befores[j]) for j in range(tiles)
         ])
 
-    for copy in early_shift:
+    for i, copy in enumerate(early_shift):
         receive(copy)
-    total5 = blocks(low + TILE, rows - 2 * TILE, final_first, total5)
+        begin, size = inner[i]
+        cut_low, cut_high = TILE * (i == 0), TILE * (i == 3)
+        total5 = blocks(begin + cut_low, size - cut_low - cut_high, final_first, total5)
 
     @pl.when(jnp.logical_not(first))
     def _():
@@ -724,34 +767,35 @@
     for r in (low, high - TILE):
         total5 = final_first(r, total5)
 
-    parts.append(total5)
-    for level, value in enumerate(parts):
-        tile[level:level + 1, :] = jnp.sum(value, axis=0, keepdims=True)
-    for level in range(len(parts), TILE):
-        tile[level:level + 1, :] = jnp.zeros((1, LANES), jnp.float32)
-
-    def exchange(count, own, source, slots, copier, send_sems, recv_sems):
-        slots[pl.ds(own, 1)] = source[...][None]
-        sent = [
-            copier(source, slots.at[own], send_sems.at[i], recv_sems.at[own], lax.rem(own + i, count))
-            for i in range(1, count)
-        ]
-        for copy in sent:
-            copy.start()
-        for i in range(1, count):
-            other = lax.rem(own + i, count)
-            copier(source, slots.at[other], send_sems.at[i], recv_sems.at[other], other).wait_recv()
-        for copy in sent:
-            copy.wait_send()
-        total = slots[0]
-        for i in range(1, count):
-            total = total + slots[i]
-        return total
-
-    total = exchange(devices, me, tile, gathered, tm_copy, ns_sem, nr_sem)
-    tile[...] = total
-    total = exchange(strips, strip, tile, gathered_z, space_copy, ms_sem, mr_sem)
-    summed = jnp.sum(total, axis=1, keepdims=True)
+    final_row[...] = jnp.sum(total5, axis=0, keepdims=True)
+
+    def final_slot(t, z):
+        return t * strips + z
+
+    own_slot = final_slot(me, strip)
+    final_sent = []
+    for i in range(1, devices * strips):
+        t, z = lax.rem(me + i // strips, devices), lax.rem(strip + i % strips, strips)
+        final_sent.append(pltpu.make_async_remote_copy(
+            src_ref=final_row, dst_ref=final_rows.at[own_slot], send_sem=fs_sem.at[i], recv_sem=fr_sem.at[own_slot],
+            device_id={"tm": t, "space": z}, device_id_type=DEVICE,
+        ))
+    for copy in final_sent:
+        copy.start()
+    final_rows[pl.ds(own_slot, 1)] = final_row[...][None]
+    end_strip_sum()
+    for i in range(1, devices * strips):
+        t, z = lax.rem(me + i // strips, devices), lax.rem(strip + i % strips, strips)
+        spot = final_rows.at[final_slot(t, z)]
+        pltpu.make_async_remote_copy(
+            src_ref=spot, dst_ref=spot, send_sem=fs_sem.at[i], recv_sem=fr_sem.at[final_slot(t, z)],
+            device_id={"tm": t, "space": z}, device_id_type=DEVICE,
+        ).wait_recv()
+    total = final_rows[0]
+    for i in range(1, devices * strips):
+        total = total + final_rows[i]
+    tile[LEVELS:LEVELS + 1, :] = total
+    summed = jnp.sum(tile[...], axis=1, keepdims=True)
     norms_out[...] = jnp.broadcast_to(jnp.sqrt(summed * (1.0 / cells)), (TILE, LANES))
 
     @pl.when(jnp.logical_not(last))
@@ -759,7 +803,7 @@
         for copy in guess_shift + early_shift:
             copy.wait_send()
 
-    for copy in handed + back_own:
+    for copy in handed + swaps + back_own + final_sent:
         copy.wait_send()
     for i in range(3):
         @pl.when(has_before[i])
@@ -800,9 +844,12 @@
         pltpu.VMEM((TILE, LANES), jnp.float32),
         pltpu.VMEM((devices, TILE, LANES), jnp.float32),
         pltpu.VMEM((strips, TILE, LANES), jnp.float32),
+        pltpu.VMEM((1, LANES), jnp.float32),
+        pltpu.VMEM((devices * strips, 1, LANES), jnp.float32),
         dma((5, tiles)), dma((7, 2)), dma((7, 2)), dma((3, 4)), dma((3, 4)), dma((devices,)), dma((devices,)), dma,
-        dma((2, devices)), dma((2, devices)), dma((2,)), dma((devices,)),
+        dma((devices,)), dma((devices,)), dma((2, devices)), dma((2, devices)), dma((2,)), dma((devices,)),
         dma((devices,)), dma((devices,)), dma((strips,)), dma((strips,)),
+        dma((devices * strips,)), dma((devices * strips,)),
     ]
     any_space = pl.BlockSpec(memory_space=pl.ANY)
     result, norms = pl.pallas_call(

time: 91.9 us -> 88.1 us (0.959)
  Pallas kernels: 89.1 us -> 85.3 us
    pallas_call x1, Pallas kernels: 89.1 us -> 85.3 us  [fast_body(): pl.pallas_call(functools.partial(cycle_kernel, strips, devices, cells), o...]
where the time goes in v4:
time: 88.1 us; the launch traced here: 87.9 us
  Pallas kernels  85.3 us (97%)
  local copies, waits for them, and re-layouts  1.95 us (2%)
    pallas_call x1, Pallas kernels, fast_body(): pl.pallas_call(functools.partial(cycle_kernel, strips, devices, cells), o...  85.3 us

profile of v4, /device:TPU:0, one launch (start us, length us, event | category | flops | bytes accessed | tf_op | source)
XLA Modules:
  0.0 87.9 jit_solution(5250473884678075005)
XLA Ops:
  0.6 85.3 %shard_map.50 = (f32[2,256,1024]{2,1,0:T(8,128)S(1)}, f32[8,128]{1,0:T(8,128)}) custom-call(f32[2,256,1024]{2,1,0:T(8,128)} %rhs_in.1, f32[2,256,1024]{2,1,0:T(8,128)} %guess_in.1, f32[256,1024]{1,0:T(8,128)} %diff_in.1), custom_call_target="tpu_custom_call" | custom-call | tf_op jit(solution)/shard_map/pallas_call | solution.py:855
  85.9 0.0 copy-start
  86.0 1.3 %copy.6 = f32[2,256,1024]{2,1,0:T(8,128)} copy(f32[2,256,1024]{2,1,0:T(8,128)S(1)} %get-tuple-element.6) | data formatting | bytes 4194304
  87.3 0.0 copy-done
  87.3 0.6 slice_reduce_fusion
Async XLA Ops:
  85.9 1.3 %copy-start = (f32[8,128]{1,0:T(8,128)S(1)}, f32[8,128]{1,0:T(8,128)}, u32[]{:S(2)}) copy-start(f32[8,128]{1,0:T(8,128)} %get-tuple-element.5) | copy-start | bytes 12292

commit v5 on v4

--- a/solution.py
+++ b/solution.py
@@ -124,7 +124,7 @@
 TILE = 8
 EDGE = 2 * TILE
 BLOCK = 64
-EARLY = 2
+EARLY = 5
 LANES = 128
 
 
@@ -317,7 +317,8 @@
 
     guess_shift = shift(0, guess.at[1], guess_e, guess_parts)
     v0_shift = shift(1, v0.at[1], v0_e, inner)
-    early_shift = shift(2, early, early_e, inner)
+    early_parts = [(low + rows // 8 * j, rows // 8) for j in range(8)]
+    early_shift = shift(2, early, early_e, early_parts)
 
     for copy in loads[0]:
         copy.wait()
@@ -680,9 +681,6 @@
 
         absorb(place_tiles(k))
     start_halo(v1f_halo)
-    end_time_sum()
-    end_strip_sum = begin_sum(strips, strip, gathered_z, space_copy, ms_sem, mr_sem)
-
     def ascend_last(r, carry, store=True):
         mids, totals = stencil(v0.at[1], r)
         for j in range(tiles):
@@ -700,14 +698,17 @@
             sol[0, j, at(r), :] = keep_share * mids[j] + weights[0, j, at(r), :] * inner_sum
         return carry
 
-    blocks(low + TILE, rows - 2 * TILE, ascend_last)
+    def ascend_inside(r, carry):
+        return ascend_first(r, ascend_last(r, carry))
+
+    blocks(low + TILE, rows - 2 * TILE, ascend_inside)
     finish_halo(v1f_halo)
     absorb(halo_tiles)
     for r in (low, high - TILE):
-        ascend_last(r, 0)
+        ascend_inside(r, 0)
     for r in halo_tiles:
         ascend_last(r, 0, False)
-    blocks(low - TILE, rows + 2 * TILE, ascend_first)
+        ascend_first(r, 0)
 
     def final_last(r, carry):
         mids, totals = stencil(sol.at[1], r)
@@ -716,6 +717,9 @@
         return carry
 
     blocks(low, rows, final_last)
+    end_time_sum()
+    end_strip_sum = begin_sum(strips, strip, gathered_z, space_copy, ms_sem, mr_sem)
+
     def complete(r, carry):
         resid = []
         for j in range(tiles):
@@ -753,8 +757,8 @@
 
     for i, copy in enumerate(early_shift):
         receive(copy)
-        begin, size = inner[i]
-        cut_low, cut_high = TILE * (i == 0), TILE * (i == 3)
+        begin, size = early_parts[i]
+        cut_low, cut_high = TILE * (i == 0), TILE * (i == len(early_parts) - 1)
         total5 = blocks(begin + cut_low, size - cut_low - cut_high, final_first, total5)
 
     @pl.when(jnp.logical_not(first))
@@ -796,7 +800,9 @@
         total = total + final_rows[i]
     tile[LEVELS:LEVELS + 1, :] = total
     summed = jnp.sum(tile[...], axis=1, keepdims=True)
-    norms_out[...] = jnp.broadcast_to(jnp.sqrt(summed * (1.0 / cells)), (TILE, LANES))
+    roots = jnp.sqrt(summed * (1.0 / cells))
+    for level in range(LEVELS + 1):
+        norms_out[level] = roots[level, 0]
 
     @pl.when(jnp.logical_not(last))
     def _():
@@ -846,7 +852,7 @@
         pltpu.VMEM((strips, TILE, LANES), jnp.float32),
         pltpu.VMEM((1, LANES), jnp.float32),
         pltpu.VMEM((devices * strips, 1, LANES), jnp.float32),
-        dma((5, tiles)), dma((7, 2)), dma((7, 2)), dma((3, 4)), dma((3, 4)), dma((devices,)), dma((devices,)), dma,
+        dma((5, tiles)), dma((7, 2)), dma((7, 2)), dma((3, 8)), dma((3, 8)), dma((devices,)), dma((devices,)), dma,
         dma((devices,)), dma((devices,)), dma((2, devices)), dma((2, devices)), dma((2,)), dma((devices,)),
         dma((devices,)), dma((devices,)), dma((strips,)), dma((strips,)),
         dma((devices * strips,)), dma((devices * strips,)),
@@ -856,16 +862,16 @@
         functools.partial(cycle_kernel, strips, devices, cells),
         out_shape=(
             pltpu.VMEM(rhs.shape, jnp.float32),
-            jax.ShapeDtypeStruct((TILE, LANES), jnp.float32),
+            jax.ShapeDtypeStruct((LEVELS + 1,), jnp.float32),
         ),
         in_specs=[any_space] * 3,
-        out_specs=(pl.BlockSpec(memory_space=pltpu.VMEM), pl.BlockSpec(memory_space=pltpu.VMEM)),
+        out_specs=(pl.BlockSpec(memory_space=pltpu.VMEM), pl.BlockSpec(memory_space=pltpu.SMEM)),
         scratch_shapes=scratch,
         compiler_params=pltpu.CompilerParams(
             collective_id=0, has_side_effects=True, vmem_limit_bytes=67_043_328 - rhs.size * 4 - 2**17
         ),
     )(rhs, guess, diffusion)
-    return result, norms[:LEVELS + 1, 0]
+    return result, norms
 
 
 def solution(mesh):

time: 88.1 us -> 87.9 us (level)
    unnamed x3 -> x4, local copies, waits for them, and re-layouts: 1.33 us -> 1.84 us
where the time goes in v5:
time: 87.9 us; the launch traced here: 87.8 us
  Pallas kernels  85.3 us (97%)
  local copies, waits for them, and re-layouts  1.84 us (2%)
    pallas_call x1, Pallas kernels, fast_body(): pl.pallas_call(functools.partial(cycle_kernel, strips, devices, cells), o...  85.3 us
    unnamed x4, local copies, waits for them, and re-layouts  1.84 us

profile of v5, /device:TPU:0, one launch (start us, length us, event | category | flops | bytes accessed | tf_op | source)
XLA Modules:
  0.0 87.8 jit_solution(11224281942176365155)
XLA Ops:
  0.6 85.3 %shard_map.50 = (f32[2,256,1024]{2,1,0:T(8,128)S(1)}, f32[6]{0:T(128)}) custom-call(f32[2,256,1024]{2,1,0:T(8,128)} %rhs_in.1, f32[2,256,1024]{2,1,0:T(8,128)} %guess_in.1, f32[256,1024]{1,0:T(8,128)} %diff_in.1), custom_call_target="tpu_custom_call" | custom-call | tf_op jit(solution)/shard_map/pallas_call | solution.py:861
  85.9 0.0 copy-start
  85.9 1.3 %copy.7 = f32[2,256,1024]{2,1,0:T(8,128)} copy(f32[2,256,1024]{2,1,0:T(8,128)S(1)} %get-tuple-element.2) | data formatting | bytes 4194304
  87.2 0.0 copy-done
  87.2 0.5 copy.8
Async XLA Ops:
  85.9 1.3 %copy-start = (f32[6]{0:T(128)S(1)}, f32[6]{0:T(128)}, u32[]{:S(2)}) copy-start(f32[6]{0:T(128)} %get-tuple-element.7) | copy-start | bytes 76
